TPU v7x, 16 devices: a whole 2x2x2 slice. The times are simulated.
16 devices in a mesh: dp: 4 (over z, y), sh: 4 (over x, core).
Axes of the slice: x: 2, y: 2, z: 2, core: 2. Of those that a mesh axis runs over, the one named last changes fastest.
Arguments:
- k_prefill: bfloat16 [16, 7168, 8, 256], P('dp', None, 'sh'), parts along dimension 0
- v_prefill: bfloat16 [16, 7168, 8, 256], P('dp', None, 'sh'), parts along dimension 0
- lengths: int32 [16], P('dp'), parts along dimension 0
- residual: bfloat16 [16, 3584], P(('dp', 'sh')), parts along dimension 0
- norm_gain: bfloat16 [3584], replicated
- w_query: bfloat16 [3584, 4096], replicated
- w_key: bfloat16 [3584, 2048], replicated
- w_value: bfloat16 [3584, 2048], replicated
- w_out: bfloat16 [4096, 3584], replicated
Outputs:
- output 1: bfloat16 [16, 3584], P(('dp', 'sh')), parts along dimension 0
- output 2: bfloat16 [16, 4096, 8, 256], P(('dp', 'sh')), parts along dimension 0
- output 3: bfloat16 [16, 4096, 8, 256], P(('dp', 'sh')), parts along dimension 0
There are 4 independent parts. A program takes and returns all parts, laid end to end along the dimension named above; an argument that names none is the same for every part.
All inputs are finite; a program needn't handle non-finite values.
Results may differ from a plain program's by a relative error of at most 0.00415.
Values are sent between devices in bfloat16 or wider.
A program may use at most 1 GiB of HBM per device.

v0:
```python
import functools
import math

import jax
import jax.numpy as jnp
from jax import lax
from jax.experimental import pallas as pl
from jax.experimental.pallas import tpu as pltpu
from jax.sharding import PartitionSpec as P


WINDOW = 4096
THETA = 10000.0
EPS = 1e-5
LANES = 128
BLOCK = 256
DEPTH = 6
FLIGHT = 16
ZEROS = 32
VMEM_BYTES = 67043328
LOW = 2560
K_CHUNKS = (512, 2048)
V_CHUNKS = (1792, 512, 256)
UNIT = 128
UPPER = (WINDOW - LOW) // UNIT
LANES_OF_CUT = 4
PART = 4


def build_kernel(partners, c0, lens_ref, src_ref, _, *refs):
    ways = len(partners)
    outs = refs[:ways]
    buf, other, in_sem, other_sem, out_sem = refs[ways:]
    me = lax.axis_index('sh')
    size = outs[0].shape[0]
    block = math.gcd(BLOCK, size)
    total = size // block * ways
    last = src_ref.shape[1] - block
    rows = pl.ds(0, block)

    def where(i):
        row = me ^ partners[0]
        for p, j in enumerate(partners[1:]):
            row = jnp.where(lax.rem(i, ways) == p + 1, me ^ j, row)
        return row, c0 + i // ways * block, jnp.maximum(lens_ref[row] - WINDOW, 0)

    def in_copy(i, row, start):
        slot = lax.rem(i, FLIGHT)
        return pltpu.make_async_copy(src_ref.at[row, pl.ds(start, block)], buf.at[slot, rows], in_sem.at[slot])

    def other_copy(row, start):
        return pltpu.make_async_copy(src_ref.at[row, pl.ds(start, block)], other.at[rows], other_sem)

    def out_copy(i, out):
        slot = lax.rem(i, FLIGHT)
        return pltpu.make_async_copy(buf.at[slot, rows], out.at[pl.ds(i // ways * block, block)], out_sem.at[slot])

    def start_in(i):
        row, base, wrapped = where(i)
        in_copy(i, row, jnp.where(base + block <= wrapped, jnp.minimum(base + WINDOW, last), base)).start()

    def finish(i):
        row, base, wrapped = where(i)
        slot = lax.rem(i, FLIGHT)
        in_copy(i, row, 0).wait()

        @pl.when((base < wrapped) & (base + block > wrapped))
        def _():
            copy = other_copy(row, jnp.minimum(base + WINDOW, last))
            copy.start()
            copy.wait()

            @pl.loop(0, wrapped - base)
            def _(s):
                buf[slot, s] = other[s]

        for p, out in enumerate(outs):
            @pl.when(lax.rem(i, ways) == p)
            def _():
                out_copy(i, out).start()

    @pl.loop(0, min(FLIGHT - 1, total))
    def _(i):
        start_in(i)

    @pl.loop(0, total)
    def _(i):
        finish(i)
        ahead = i + FLIGHT - 1

        @pl.when(ahead < total)
        def _():
            @pl.when(i >= 1)
            def _():
                out_copy(i - 1, outs[0]).wait()

            start_in(ahead)

    @pl.loop(max(total - FLIGHT, 0), total)
    def _(i):
        out_copy(i, outs[0]).wait()


def build(lengths, src, partners, c0, size, after):
    tile = src.shape[2:]
    return pl.pallas_call(
        functools.partial(build_kernel, partners, c0),
        out_shape=[jax.ShapeDtypeStruct((size,) + tile, src.dtype) for _ in partners],
        in_specs=[pl.BlockSpec(memory_space=pltpu.SMEM), pl.BlockSpec(memory_space=pltpu.HBM), pl.BlockSpec(memory_space=pl.ANY)],
        out_specs=[pl.BlockSpec(memory_space=pltpu.HBM)] * len(partners),
        scratch_shapes=[
            pltpu.VMEM((FLIGHT, BLOCK) + tile, src.dtype),
            pltpu.VMEM((BLOCK,) + tile, src.dtype),
            pltpu.SemaphoreType.DMA((FLIGHT,)),
            pltpu.SemaphoreType.DMA,
            pltpu.SemaphoreType.DMA((FLIGHT,)),
        ],
        compiler_params=pltpu.CompilerParams(vmem_limit_bytes=VMEM_BYTES),
        cost_estimate=pl.CostEstimate(flops=10 ** 9, bytes_accessed=size * 4096, transcendentals=0),
    )(lengths, src, after)


def place_kernel(c0, size, has_prev, lens_ref, fresh_ref, own, near, far0, far1, *refs):
    out = refs[1] if has_prev else refs[0]
    buf, zeros, in_sem, out_sem = refs[-4:]
    me = lax.axis_index('sh')
    new_slot = lax.rem(lens_ref[me], WINDOW)
    filled = jnp.minimum(lens_ref[me], WINDOW)
    block = math.gcd(BLOCK, size)
    count = size // block
    rows = pl.ds(0, block)

    @pl.when(filled < c0 + size)
    def _():
        zeros[...] = jnp.zeros_like(zeros)

    def empty(i):
        base = c0 + i * block
        return (base >= filled) & ((new_slot < base) | (new_slot >= base + block))

    def in_copies(i):
        slot = lax.rem(i, DEPTH)
        local = pl.ds(i * block, block)
        whole = pl.ds(c0 + i * block, block)
        views = (own.at[whole], near.at[whole], far0.at[local], far1.at[local])
        return [
            pltpu.make_async_copy(view, buf.at[slot, rows, :, me ^ j], in_sem.at[slot, j])
            for j, view in enumerate(views)
        ]

    def out_copy(i):
        slot = lax.rem(i, DEPTH)
        return pltpu.make_async_copy(buf.at[slot, rows], out.at[pl.ds(c0 + i * block, block)], out_sem.at[slot])

    def start_in(i):
        @pl.when(jnp.logical_not(empty(i)))
        def _():
            for copy in in_copies(i):
                copy.start()

    def finish(i):
        slot = lax.rem(i, DEPTH)
        base = c0 + i * block

        @pl.when(empty(i))
        def _():
            for part in range(block // ZEROS):
                pltpu.make_async_copy(zeros, out.at[pl.ds(base + part * ZEROS, ZEROS)], out_sem.at[slot]).start()

        @pl.when(jnp.logical_not(empty(i)))
        def _():
            for copy in in_copies(i):
                copy.wait()

            @pl.when(base + block > filled)
            def _():
                @pl.loop(jnp.maximum(filled - base, 0), block)
                def _(s):
                    buf[slot, s] = zeros[0]

            spot = new_slot - base

            @pl.when((spot >= 0) & (spot < block))
            def _():
                buf[slot, spot] = fresh_ref[...]

            out_copy(i).start()

    for i in range(min(DEPTH - 1, count)):
        start_in(jnp.int32(i))

    @pl.loop(0, count)
    def _(i):
        finish(i)
        ahead = i + DEPTH - 1

        @pl.when(ahead < count)
        def _():
            @pl.when(i >= 1)
            def _():
                out_copy(i - 1).wait()

            start_in(ahead)

    for i in range(max(count - DEPTH, 0), count):
        out_copy(jnp.int32(i)).wait()


def used_units(length):
    return (jnp.maximum(jnp.minimum(length, WINDOW) - LOW, 0) + UNIT - 1) // UNIT


def lane_counts(lens, half, lane):
    counts = []
    for g in range(LANES_OF_CUT):
        total = 2 * (used_units(lens(g, 2 * half)) + used_units(lens(g, 2 * half + 1)))
        counts.append((total + 3 - lane) // LANES_OF_CUT)
    return counts


def stream(count, depth, start_in, finish_in, start_out, wait_out):
    @pl.loop(0, jnp.minimum(count, depth - 1))
    def _(i):
        start_in(i)

    @pl.loop(0, count)
    def _(i):
        finish_in(i)
        start_out(i)
        ahead = i + depth - 1

        @pl.when(ahead < count)
        def _():
            @pl.when(i >= 1)
            def _():
                wait_out(i - 1)

            start_in(ahead)

    @pl.loop(jnp.maximum(count - depth, 0), count)
    def _(i):
        wait_out(i)


def pick(index, refs, action):
    for k, ref in enumerate(refs):
        @pl.when(index == k)
        def _():
            action(ref)


def deal_kernel(lens_ref, k_ref, v_ref, _, *refs):
    outs = refs[:LANES_OF_CUT]
    buf, other, in_sem, other_sem, out_sem = refs[LANES_OF_CUT:]
    depth = buf.shape[0]
    g = lax.axis_index('dp')
    row0 = 2 * (1 - lax.axis_index('sh') // 2)
    last = k_ref.shape[1] - UNIT
    counts = [used_units(lens_ref[row0 + c]) for c in (0, 1)]
    both = counts[0] + counts[1]

    def where(u):
        w = u - jnp.where(u >= both, both, 0)
        second = w >= counts[0]
        row = row0 + jnp.where(second, 1, 0)
        return u >= both, row, LOW + (w - jnp.where(second, counts[0], 0)) * UNIT, jnp.maximum(lens_ref[row] - WINDOW, 0)

    def in_copy(u, src, row, start):
        slot = lax.rem(u, depth)
        return pltpu.make_async_copy(src.at[row, pl.ds(start, UNIT)], buf.at[slot], in_sem.at[slot])

    def start_in(u):
        value, row, base, wrapped = where(u)
        start = jnp.where(base + UNIT <= wrapped, jnp.minimum(base + WINDOW, last), base)
        pick(jnp.where(value, 1, 0), (k_ref, v_ref), lambda src: in_copy(u, src, row, start).start())

    def finish_in(u):
        value, row, base, wrapped = where(u)
        slot = lax.rem(u, depth)
        in_copy(u, k_ref, row, 0).wait()

        @pl.when((base < wrapped) & (base + UNIT > wrapped))
        def _():
            def fetch(src):
                copy = pltpu.make_async_copy(src.at[row, pl.ds(jnp.minimum(base + WINDOW, last), UNIT)], other, other_sem)
                copy.start()
                copy.wait()

            pick(jnp.where(value, 1, 0), (k_ref, v_ref), fetch)

            @pl.loop(0, wrapped - base)
            def _(s):
                buf[slot, s] = other[s]

    def out_copy(u, out):
        slot = lax.rem(u, depth)
        return pltpu.make_async_copy(buf.at[slot], out.at[pl.ds(u // LANES_OF_CUT * UNIT, UNIT)], out_sem.at[slot])

    stream(2 * both, depth, start_in, finish_in,
           lambda u: pick(lax.rem(u, LANES_OF_CUT) ^ g, outs, lambda out: out_copy(u, out).start()),
           lambda u: out_copy(u, outs[0]).wait())


def compact_kernel(back, lens_ref, *refs):
    parts = LANES_OF_CUT * UPPER // PART
    sources = refs[:parts if back else LANES_OF_CUT]
    outs = refs[len(sources):len(sources) + (LANES_OF_CUT if back else parts)]
    buf, in_sem, out_sem = refs[-3:]
    depth = buf.shape[0]
    lane = lax.axis_index('dp')
    half = lax.axis_index('sh') // 2
    counts = lane_counts(lambda g, row: lens_ref[4 * g + row], half if back else 1 - half, lane)
    ends = [counts[0]]
    for count in counts[1:]:
        ends.append(ends[-1] + count)

    def spot(i):
        g = jnp.int32(0)
        first = jnp.int32(0)
        for k in range(LANES_OF_CUT - 1):
            g = jnp.where(i >= ends[k], k + 1, g)
            first = jnp.where(i >= ends[k], ends[k], first)
        container, dense = (g ^ lane, i - first), (i // PART, lax.rem(i, PART))
        return (dense, container) if back else (container, dense)

    def in_copy(i, src, at):
        slot = lax.rem(i, depth)
        return pltpu.make_async_copy(src.at[pl.ds(at * UNIT, UNIT)], buf.at[slot], in_sem.at[slot])

    def out_copy(i, out, at):
        slot = lax.rem(i, depth)
        return pltpu.make_async_copy(buf.at[slot], out.at[pl.ds(at * UNIT, UNIT)], out_sem.at[slot])

    def start_in(i):
        which, at = spot(i)[0]
        pick(which, sources, lambda src: in_copy(i, src, at).start())

    def start_out(i):
        which, at = spot(i)[1]
        pick(which, outs, lambda out: out_copy(i, out, at).start())

    stream(ends[-1], depth, start_in, lambda i: in_copy(i, sources[0], 0).wait(), start_out,
           lambda i: out_copy(i, outs[0], 0).wait())


def place_upper_kernel(values, lens_ref, fresh_ref, own, near, *refs):
    mine, others = refs[:LANES_OF_CUT], refs[LANES_OF_CUT:2 * LANES_OF_CUT]
    out, buf, zeros, in_sem, out_sem = refs[2 * LANES_OF_CUT + 1:]
    depth = buf.shape[0]
    g = lax.axis_index('dp')
    me = lax.axis_index('sh')
    core = lax.rem(me, 2)
    length = lens_ref[me]
    new_slot = lax.rem(length, WINDOW)
    filled = jnp.minimum(length, WINDOW)
    used = used_units(length)
    sibling = used_units(lens_ref[me ^ 1])
    start = jnp.where(core == 1, sibling, 0) + (used + sibling if values else 0)

    zeros[...] = jnp.zeros_like(zeros)

    def in_copy(b, j, view):
        slot = lax.rem(b, depth)
        return pltpu.make_async_copy(view, buf.at[slot, :, :, me ^ j], in_sem.at[slot, j])

    def start_in(b):
        @pl.when(b < used)
        def _():
            u = start + b
            at = pl.ds(u // LANES_OF_CUT * UNIT, UNIT)
            which = lax.rem(u, LANES_OF_CUT) ^ g
            here = pl.ds(LOW + b * UNIT, UNIT)
            in_copy(b, 0, own.at[here]).start()
            in_copy(b, 1, near.at[here]).start()
            pick(which, mine, lambda src: in_copy(b, 2, src.at[at]).start())
            pick(which, others, lambda src: in_copy(b, 3, src.at[at]).start())

    def finish_in(b):
        slot = lax.rem(b, depth)
        base = LOW + b * UNIT

        @pl.when(b < used)
        def _():
            for j in range(4):
                in_copy(b, j, own.at[pl.ds(0, UNIT)]).wait()

        spot = new_slot - base
        inside = (spot >= 0) & (spot < UNIT)

        @pl.when((base + UNIT > filled) & ((b < used) | inside))
        def _():
            @pl.loop(jnp.maximum(filled - base, 0), UNIT)
            def _(s):
                buf[slot, s] = zeros[0]

        @pl.when(inside)
        def _():
            buf[slot, spot] = fresh_ref[...]

    def out_copy(b):
        slot = lax.rem(b, depth)
        return pltpu.make_async_copy(buf.at[slot], out.at[pl.ds(LOW + b * UNIT, UNIT)], out_sem.at[slot])

    def start_out(b):
        slot = lax.rem(b, depth)
        base = LOW + b * UNIT
        blank = (b >= used) & ((new_slot < base) | (new_slot >= base + UNIT))

        @pl.when(blank)
        def _():
            for part in range(UNIT // ZEROS):
                pltpu.make_async_copy(zeros, out.at[pl.ds(base + part * ZEROS, ZEROS)], out_sem.at[slot]).start()

        @pl.when(jnp.logical_not(blank))
        def _():
            out_copy(b).start()

    stream(jnp.int32(UPPER), depth, start_in, finish_in, start_out, lambda b: out_copy(b).wait())


def local_call(kernel, scalars, vectors, arrays, outs, scratch, aliases, moved):
    hbm = pl.BlockSpec(memory_space=pltpu.HBM)
    return pl.pallas_call(
        kernel,
        out_shape=outs,
        in_specs=[pl.BlockSpec(memory_space=pltpu.SMEM)] * len(scalars) + [pl.BlockSpec(memory_space=pltpu.VMEM)] * len(vectors) + [hbm] * len(arrays),
        out_specs=jax.tree.map(lambda _: hbm, outs),
        scratch_shapes=scratch,
        input_output_aliases=aliases,
        compiler_params=pltpu.CompilerParams(vmem_limit_bytes=VMEM_BYTES),
        cost_estimate=pl.CostEstimate(flops=10 ** 9, bytes_accessed=moved, transcendentals=0),
    )(*scalars, *vectors, *arrays)


def deal(lengths, k_src, v_src, after):
    tile, dtype, depth = k_src.shape[2:], k_src.dtype, 2 * FLIGHT
    return local_call(
        deal_kernel, [lengths], [], [k_src, v_src, after],
        [jax.ShapeDtypeStruct((UPPER * UNIT,) + tile, dtype)] * LANES_OF_CUT,
        [pltpu.VMEM((depth, UNIT) + tile, dtype), pltpu.VMEM((UNIT,) + tile, dtype), pltpu.SemaphoreType.DMA((depth,)), pltpu.SemaphoreType.DMA, pltpu.SemaphoreType.DMA((depth,))],
        {}, 16 << 20)


def compact(every_length, arrays, back):
    tile, dtype, depth = arrays[0].shape[1:], arrays[0].dtype, 2 * FLIGHT
    many, size = (LANES_OF_CUT, UPPER) if back else (LANES_OF_CUT * UPPER // PART, PART)
    return local_call(
        functools.partial(compact_kernel, back), [every_length], [], arrays,
        [jax.ShapeDtypeStruct((size * UNIT,) + tile, dtype)] * many,
        [pltpu.VMEM((depth, UNIT) + tile, dtype), pltpu.SemaphoreType.DMA((depth,)), pltpu.SemaphoreType.DMA((depth,))],
        {}, 16 << 20)


def place_upper(values, lengths, fresh, own, near, mine, others, prev):
    halves, pair, lanes = own.shape[1:]
    depth = 8
    return local_call(
        functools.partial(place_upper_kernel, values), [lengths], [fresh], [own, near, *mine, *others, prev],
        jax.ShapeDtypeStruct(prev.shape, prev.dtype),
        [pltpu.VMEM((depth, UNIT, halves, 4, pair, lanes), own.dtype), pltpu.VMEM((ZEROS, halves, 4, pair, lanes), own.dtype), pltpu.SemaphoreType.DMA((depth, 4)), pltpu.SemaphoreType.DMA((depth,))],
        {4 + 2 * LANES_OF_CUT: 0}, 16 << 20)


def place(lengths, fresh, own, near, far0, far1, c0, prev):
    size = far0.shape[0]
    hbm = pl.BlockSpec(memory_space=pltpu.HBM)
    operands = [lengths, fresh, own, near, far0, far1]
    if prev is not None:
        operands.append(prev)
    halves, pair, lanes = own.shape[1:]
    return pl.pallas_call(
        functools.partial(place_kernel, c0, size, prev is not None),
        out_shape=jax.ShapeDtypeStruct((WINDOW, halves, 4, pair, lanes), own.dtype),
        in_specs=[pl.BlockSpec(memory_space=pltpu.SMEM), pl.BlockSpec(memory_space=pltpu.VMEM)] + [hbm] * (len(operands) - 2),
        out_specs=hbm,
        scratch_shapes=[
            pltpu.VMEM((DEPTH, BLOCK, halves, 4, pair, lanes), own.dtype),
            pltpu.VMEM((ZEROS, halves, 4, pair, lanes), own.dtype),
            pltpu.SemaphoreType.DMA((DEPTH, 4)),
            pltpu.SemaphoreType.DMA((DEPTH,)),
        ],
        input_output_aliases={} if prev is None else {6: 0},
        compiler_params=pltpu.CompilerParams(vmem_limit_bytes=VMEM_BYTES),
        cost_estimate=pl.CostEstimate(flops=10 ** 9, bytes_accessed=size * 8192, transcendentals=0),
    )(*operands)


def rotate(heads, positions):
    head_dim = heads.shape[-1]
    half_dim = head_dim // 2
    inv_freq = THETA ** (-2.0 * jnp.arange(half_dim, dtype=jnp.float32) / head_dim)
    angles = positions.astype(jnp.float32).reshape(positions.shape + (1,) * (heads.ndim - 1)) * inv_freq
    cos_part = jnp.cos(angles)
    sin_part = jnp.sin(angles)
    first_half = heads[..., :half_dim].astype(jnp.float32)
    second_half = heads[..., half_dim:].astype(jnp.float32)
    return jnp.concatenate([first_half * cos_part - second_half * sin_part, second_half * cos_part + first_half * sin_part], axis=-1).astype(jnp.bfloat16)


def normalize(residual, norm_gain):
    resid_f32 = residual.astype(jnp.float32)
    inv_rms = lax.rsqrt(jnp.mean(resid_f32 * resid_f32, axis=-1, keepdims=True) + EPS)
    return (resid_f32 * inv_rms * norm_gain.astype(jnp.float32)).astype(jnp.bfloat16)


def project(normed, weight):
    return jnp.dot(normed, weight, preferred_element_type=jnp.float32).astype(jnp.bfloat16)


def split_lanes(array):
    halves = array.shape[-1] // LANES
    return jnp.swapaxes(array.reshape(array.shape[:-1] + (halves, LANES)), -3, -2)


def attend_heads(q_heads, k_new, v_new, k_prefill, v_prefill, lengths):
    scale = q_heads.shape[-1] ** 0.5
    positions = jnp.arange(k_prefill.shape[1], dtype=jnp.int32)[None, :]
    live = (positions < lengths[:, None]) & (positions > lengths[:, None] - WINDOW)
    scores = jnp.einsum('rkgd,rwkd->rkgw', q_heads, k_prefill, preferred_element_type=jnp.float32) / scale
    scores = jnp.where(live[:, None, None, :], scores, -jnp.inf)
    new_score = jnp.sum(q_heads.astype(jnp.float32) * k_new.astype(jnp.float32)[:, :, None, :], axis=-1, keepdims=True) / scale
    top = jnp.maximum(jnp.max(scores, axis=-1, keepdims=True), new_score)
    exp_scores = jnp.exp(scores - top)
    new_exp = jnp.exp(new_score - top)
    total = jnp.sum(exp_scores, axis=-1, keepdims=True) + new_exp
    weights = (exp_scores / total).astype(jnp.bfloat16)
    new_weight = (new_exp / total).astype(jnp.bfloat16)
    mixed = jnp.einsum('rkgw,rwkd->rkgd', weights, v_prefill, preferred_element_type=jnp.float32)
    mixed = mixed + new_weight.astype(jnp.float32) * v_new.astype(jnp.float32)[:, :, None, :]
    return mixed.astype(jnp.bfloat16)


def solution(mesh):
    group = mesh.shape['sh']
    head_spec = P('dp', None, 'sh', None)
    row_spec = P(('dp', 'sh'))
    full_spec = P(None, None)

    def swap(array, j):
        return lax.ppermute(array, 'sh', [(i, i ^ j) for i in range(group)])

    def per_device(k_prefill, v_prefill, lengths, residual, norm_gain, w_query, w_key, w_value, w_out):
        kv_heads, head_dim = k_prefill.shape[2:]
        me = lax.axis_index('sh')
        by_row = jnp.arange(group, dtype=jnp.int32) ^ me

        all_resid = jnp.concatenate([residual] + [swap(residual, j) for j in range(1, group)], axis=0)
        all_resid = jnp.take(all_resid, by_row, axis=0)

        k_src, v_src = split_lanes(k_prefill), split_lanes(v_prefill)

        def build_far(src, chunks, i, after):
            return build(lengths, src, (2, 3), sum(chunks[:i]), chunks[i], after)

        def send_far(built):
            return [swap(a, j) for a, j in zip(built, (2, 3))]

        def shift(array, d):
            return lax.ppermute(array, 'dp', [(g, g ^ d) for g in range(LANES_OF_CUT)])

        every_length = jnp.stack([lengths] + [shift(lengths, d) for d in range(1, LANES_OF_CUT)])
        every_length = jnp.take(every_length, jnp.arange(LANES_OF_CUT, dtype=jnp.int32) ^ lax.axis_index('dp'), axis=0).reshape(-1)

        k_first = build_far(k_src, K_CHUNKS, 0, lengths)
        k_far = [send_far(k_first)]
        dealt = deal(lengths, k_src, v_src, k_first[0])
        k_second = build_far(k_src, K_CHUNKS, 1, dealt[0])
        dealt = [dealt[0]] + [shift(a, d + 1) for d, a in enumerate(dealt[1:])]
        k_far.append(send_far(k_second))
        v_built = []
        for i in range(len(V_CHUNKS)):
            v_built.append(build_far(v_src, V_CHUNKS, i, (k_second if i == 0 else v_built[-1])[0]))

        normed = normalize(all_resid, norm_gain)
        kv_width = kv_heads * head_dim
        q_width = w_query.shape[1] // group
        q_heads = project(normed, lax.dynamic_slice_in_dim(w_query, me * q_width, q_width, axis=1))
        q_heads = rotate(q_heads.reshape(group, kv_heads, q_width // kv_width, head_dim), lengths)
        k_new = project(normed, lax.dynamic_slice_in_dim(w_key, me * kv_width, kv_width, axis=1))
        v_new = project(normed, lax.dynamic_slice_in_dim(w_value, me * kv_width, kv_width, axis=1))
        k_new = rotate(k_new.reshape(group, kv_heads, head_dim), lengths)
        v_new = v_new.reshape(group, kv_heads, head_dim)
        mixed = attend_heads(q_heads, k_new, v_new, k_prefill, v_prefill, lengths).reshape(group, q_width)
        mixed = jnp.concatenate([mixed, k_new.reshape(group, kv_width), v_new.reshape(group, kv_width)], axis=1)
        mixed = jnp.take(mixed, by_row, axis=0)
        mine = [mixed[:1]] + [swap(mixed[j:j + 1], j) for j in range(1, group)]

        parts = compact(every_length, dealt, False)
        parts, v_built = lax.optimization_barrier((parts, v_built))
        by_group = every_length.reshape(LANES_OF_CUT, group)
        level = jnp.int32(0)
        for half in range(2):
            for lane in range(LANES_OF_CUT):
                level = jnp.maximum(level, sum(lane_counts(lambda g, row: by_group[g, row], half, lane)))

        def cross(count):
            def branch(*arrays):
                return [lax.ppermute(a, 'sh', [(i, i ^ 2) for i in range(group)]) if i < count else a for i, a in enumerate(arrays)]

            return branch

        parts = lax.switch((level + PART - 1) // PART, [cross(count) for count in range(len(parts) + 1)], *parts)

        v_far = [send_far(built) for built in v_built]
        dealt = compact(every_length, parts, True)
        dealt = [dealt[0]] + [shift(a, d + 1) for d, a in enumerate(dealt[1:])]
        others = [swap(a, 1) for a in dealt]
        k_own, k_near = build(lengths, k_src, (0, 1), 0, WINDOW, parts[0])
        k_near = swap(k_near, 1)
        v_own, v_near = build(lengths, v_src, (0, 1), 0, WINDOW, parts[0])
        v_near = swap(v_near, 1)

        mine = jnp.take(jnp.concatenate(mine, axis=0), by_row, axis=0)
        attn_out = mine[:, :q_width].reshape(1, group * q_width)
        resid_out = (residual.astype(jnp.float32) + jnp.dot(attn_out, w_out, preferred_element_type=jnp.float32)).astype(jnp.bfloat16)

        k_fresh = mine[:, q_width:q_width + kv_width].reshape(1, group * kv_heads, head_dim)
        v_fresh = mine[:, q_width + kv_width:].reshape(1, group * kv_heads, head_dim)

        def cache(fresh, own, near, far, values):
            fresh = split_lanes(fresh[0])
            fresh = fresh.reshape(fresh.shape[0], group, kv_heads, LANES)
            out, c0 = None, 0
            for far0, far1 in far:
                if values and c0 + far0.shape[0] == LOW:
                    out = place_upper(values, lengths, fresh, own, near, dealt, others, out)
                out = place(lengths, fresh, own, near, far0, far1, c0, out)
                c0 += far0.shape[0]
            if not values:
                out = place_upper(values, lengths, fresh, own, near, dealt, others, out)
            return jnp.transpose(out, (0, 2, 3, 1, 4)).reshape(1, WINDOW, group * kv_heads, head_dim)

        return resid_out, cache(k_fresh, k_own, k_near, k_far, False), cache(v_fresh, v_own, v_near, v_far, True)

    return jax.shard_map(per_device, mesh=mesh, in_specs=(head_spec, head_spec, P('dp'), P(('dp', 'sh'), None), P(None), full_spec, full_spec, full_spec, full_spec), out_specs=(P(('dp', 'sh'), None), row_spec, row_spec), check_vma=False)
```

profile of v0, /device:TPU:0, one launch (start us, length us, event | category | flops | bytes accessed | tf_op | source)
XLA Modules:
  0.0 479.3 jit_solution(17845016430005950778)
XLA Ops:
  3.5 4.2 shard_map.113
  7.7 5.2 %collective-permute-start.87 = (bf16[1536,2,2,128]{3,2,1,0:T(2,128)(2,1)}, bf16[1536,2,2,128]{3,2,1,0:T(2,128)(2,1)}, u32[]{:S(2)}, u32[]{:S(2)}) collective-permute-start(bf16[1536,2,2,128]{3,2,1,0:T(2,128)(2,1)} %get-tuple-element.526), channel_id=1, source_target_pairs={{0,4},{4,0},{8,12},{12,8},{1,5},{5,1},{9,13},{13,9},{2,6},{6,2},{1... | collective-permute-start | bytes 4718600 | tf_op jit(solution)/shard_map/ppermute | solution.py:559
  17.9 5.7 %shard_map.115 = (bf16[2048,2,2,128]{3,2,1,0:T(2,128)(2,1)}, bf16[2048,2,2,128]{3,2,1,0:T(2,128)(2,1)}) custom-call(s32[4]{0:T(128)} %lens_ref.29, bf16[4,7168,2,2,128]{4,3,2,1,0:T(2,128)(2,1)} %bitcast.59, bf16[1536,2,2,128]{3,2,1,0:T(2,128)(2,1)} %get-tuple-element.525.refs_0_._), custom_call_target="tpu_custom_call" | custom-call | flops 1000000000 | bytes 8388608 | tf_op jit(solution)/shard_map/pallas_call | solution.py:106
  27.7 4.4 shard_map.117
  34.9 46.4 %collective-permute-done.86 = s32[4]{0:T(128)} collective-permute-done((s32[4]{0:T(128)}, s32[4]{0:T(128)}, u32[]{:S(2)}, u32[]{:S(2)}) %collective-permute-start.86) | collective-permute-done | bytes 48 | tf_op jit(solution)/shard_map/ppermute | solution.py:559
  99.3 4.9 %shard_map.114 = (bf16[512,2,2,128]{3,2,1,0:T(2,128)(2,1)}, bf16[512,2,2,128]{3,2,1,0:T(2,128)(2,1)}, bf16[512,2,2,128]{3,2,1,0:T(2,128)(2,1)}, bf16[512,2,2,128...) custom-call(s32[16]{0:T(128)} %select_n.315.lens_ref, ...), custom_call_target="tpu_custom_call" | custom-call | flops 1000000000 | bytes 16777216 | tf_op jit(solution)/shard_map/pallas_call | solution.py:423
  104.3 91.6 %conditional.1 = ((bf16[512,2,2,128]{3,2,1,0:T(2,128)(2,1)}, bf16[512,2,2,128]{3,2,1,0:T(2,128)(2,1)}, bf16[512,2,2,128]{3,2,1,0:T(2,128)(2,1)}, bf16[512,2,2,12...) conditional(s32[]{:T(128)} %clamp.3, ...), branch_computations={%region_4.6_spmd, %region_5.7_spmd, %region_6.8_spmd, %region_7.9_... | conditional | bytes 37749320 | solution.py:602
  108.7 10.7 %collective-permute-done.28 = bf16[512,2,2,128]{3,2,1,0:T(2,128)(2,1)S(1)} collective-permute-done((bf16[512,2,2,128]{3,2,1,0:T(2,128)(2,1)}, bf16[512,2,2,128]{3,2,1,0:T(2,128)(2,1)S(1)}, u32[]{:S(2)}, u32[]{:S(2)}) %collective-permute-start.28) | collective-permute-done | bytes 524320 | tf_op jit(solution)/shard_map/cond/branch_8_fun/ppermute | solution.py:598
  119.6 11.0 %collective-permute-done.29 = bf16[512,2,2,128]{3,2,1,0:T(2,128)(2,1)S(1)} collective-permute-done((bf16[512,2,2,128]{3,2,1,0:T(2,128)(2,1)}, bf16[512,2,2,128]{3,2,1,0:T(2,128)(2,1)S(1)}, u32[]{:S(2)}, u32[]{:S(2)}) %collective-permute-start.29) | collective-permute-done | bytes 524320 | tf_op jit(solution)/shard_map/cond/branch_8_fun/ppermute | solution.py:598
  130.9 11.0 %collective-permute-done.30 = bf16[512,2,2,128]{3,2,1,0:T(2,128)(2,1)S(1)} collective-permute-done((bf16[512,2,2,128]{3,2,1,0:T(2,128)(2,1)}, bf16[512,2,2,128]{3,2,1,0:T(2,128)(2,1)S(1)}, u32[]{:S(2)}, u32[]{:S(2)}) %collective-permute-start.30) | collective-permute-done | bytes 524320 | tf_op jit(solution)/shard_map/cond/branch_8_fun/ppermute | solution.py:598
  144.5 8.6 %collective-permute-done.31 = bf16[512,2,2,128]{3,2,1,0:T(2,128)(2,1)S(1)} collective-permute-done((bf16[512,2,2,128]{3,2,1,0:T(2,128)(2,1)}, bf16[512,2,2,128]{3,2,1,0:T(2,128)(2,1)S(1)}, u32[]{:S(2)}, u32[]{:S(2)}) %collective-permute-start.31) | collective-permute-done | bytes 524320 | tf_op jit(solution)/shard_map/cond/branch_8_fun/ppermute | solution.py:598
  153.9 10.4 %collective-permute-done.32 = bf16[512,2,2,128]{3,2,1,0:T(2,128)(2,1)S(1)} collective-permute-done((bf16[512,2,2,128]{3,2,1,0:T(2,128)(2,1)}, bf16[512,2,2,128]{3,2,1,0:T(2,128)(2,1)S(1)}, u32[]{:S(2)}, u32[]{:S(2)}) %collective-permute-start.32) | collective-permute-done | bytes 524320 | tf_op jit(solution)/shard_map/cond/branch_8_fun/ppermute | solution.py:598
  165.2 10.4 %collective-permute-done.33 = bf16[512,2,2,128]{3,2,1,0:T(2,128)(2,1)S(1)} collective-permute-done((bf16[512,2,2,128]{3,2,1,0:T(2,128)(2,1)}, bf16[512,2,2,128]{3,2,1,0:T(2,128)(2,1)S(1)}, u32[]{:S(2)}, u32[]{:S(2)}) %collective-permute-start.33) | collective-permute-done | bytes 524320 | tf_op jit(solution)/shard_map/cond/branch_8_fun/ppermute | solution.py:598
  176.4 10.4 %collective-permute-done.34 = bf16[512,2,2,128]{3,2,1,0:T(2,128)(2,1)S(1)} collective-permute-done((bf16[512,2,2,128]{3,2,1,0:T(2,128)(2,1)}, bf16[512,2,2,128]{3,2,1,0:T(2,128)(2,1)S(1)}, u32[]{:S(2)}, u32[]{:S(2)}) %collective-permute-start.34) | collective-permute-done | bytes 524320 | tf_op jit(solution)/shard_map/cond/branch_8_fun/ppermute | solution.py:598
  187.6 7.5 %collective-permute-done.35 = bf16[512,2,2,128]{3,2,1,0:T(2,128)(2,1)S(1)} collective-permute-done((bf16[512,2,2,128]{3,2,1,0:T(2,128)(2,1)}, bf16[512,2,2,128]{3,2,1,0:T(2,128)(2,1)S(1)}, u32[]{:S(2)}, u32[]{:S(2)}) %collective-permute-start.35) | collective-permute-done | bytes 524320 | tf_op jit(solution)/shard_map/cond/branch_8_fun/ppermute | solution.py:598
  206.5 4.2 fusion.23
  210.7 18.9 %fusion.60 = (f32[4,2,2]{2,1,0:T(2,128)S(1)}, f32[4,2,2,7168]{3,2,1,0:T(2,128)S(1)}) fusion(bf16[4,7168,2,256]{3,2,1,0:T(2,128)(2,1)} %param.24, bf16[4,2,2,128]{3,2,1,0:T(2,128)(2,1)S(1)} %get-tuple-element.597, bf16[4,2,2,128]{3,2,1,0:T(2,128)(2,1)S(1)} %get-tuple-element.596, pred[4,7168]{1,0:T(4,128)(4,1)S(1)} %fusion.35), kind=kOutput, calls=%fused_computation.91 | convolution fusion | flops 59080688 | bytes 29855808 | tf_op jit(solution)/shard_map/rkgd,rwkd->rkgw/dot_general | solution.py:519
  230.3 13.3 %fusion.20 = bf16[4,2,2,256]{3,2,1,0:T(2,128)(2,1)S(1)} fusion(bf16[4,7168,2,256]{3,2,1,0:T(2,128)(2,1)} %param.25, f32[4,2,2,7168]{3,2,1,0:T(2,128)S(1)} %get-tuple-element.623, f32[4,2,2]{2,1,0:T(2,128)S(1)} %get-tuple-element.595, f32[4,2,2]{2,1,0:T(2,128)S(1)} %multiply_maximum_fusion, f32[4,2,256]{2,1,0:T(2,128)S(1)} %reshape.453, ...), kind=kOutput, calls=%fused_computation.19 | convolution fusion | flops 59076608 | bytes 29835456 | tf_op jit(solution)/shard_map/rkgw,rwkd->rkgd/dot_general | solution.py:528
  246.9 9.7 %shard_map.119 = (bf16[4096,2,2,128]{3,2,1,0:T(2,128)(2,1)}, bf16[4096,2,2,128]{3,2,1,0:T(2,128)(2,1)}) custom-call(s32[4]{0:T(128)} %lens_ref.29, bf16[4,7168,2,2,128]{4,3,2,1,0:T(2,128)(2,1)} %bitcast.60, bf16[512,2,2,128]{3,2,1,0:T(2,128)(2,1)} %get-tuple-element.560._.refs_0_), custom_call_target="tpu_custom_call" | custom-call | flops 1000000000 | bytes 16777216 | tf_op jit(solution)/shard_map/pallas_call | solution.py:106
  256.6 44.4 %collective-permute-done.83 = bf16[1,2048]{1,0:T(2,128)(2,1)} collective-permute-done((bf16[1,2048]{1,0:T(2,128)(2,1)}, bf16[1,2048]{1,0:T(2,128)(2,1)}, u32[]{:S(2)}, u32[]{:S(2)}) %collective-permute-start.83) | collective-permute-done | bytes 4128 | tf_op jit(solution)/shard_map/ppermute | solution.py:540
  301.9 9.7 %shard_map.124 = (bf16[4096,2,2,128]{3,2,1,0:T(2,128)(2,1)}, bf16[4096,2,2,128]{3,2,1,0:T(2,128)(2,1)}) custom-call(s32[4]{0:T(128)} %lens_ref.29, bf16[4,7168,2,2,128]{4,3,2,1,0:T(2,128)(2,1)} %bitcast.56, bf16[512,2,2,128]{3,2,1,0:T(2,128)(2,1)} %get-tuple-element.560._.refs_0_), custom_call_target="tpu_custom_call" | custom-call | flops 1000000000 | bytes 16777216 | tf_op jit(solution)/shard_map/pallas_call | solution.py:106
  314.0 4.2 shard_map.120
  318.2 8.2 %collective-permute-done.101.far1 = bf16[512,2,2,128]{3,2,1,0:T(2,128)(2,1)} collective-permute-done((bf16[512,2,2,128]{3,2,1,0:T(2,128)(2,1)}, bf16[512,2,2,128]{3,2,1,0:T(2,128)(2,1)}, u32[]{:S(2)}, u32[]{:S(2)}) %collective-permute-start.101) | collective-permute-done | bytes 524320 | tf_op jit(solution)/shard_map/ppermute | solution.py:540
  331.6 11.9 %collective-permute-done.105.far0 = bf16[512,2,2,128]{3,2,1,0:T(2,128)(2,1)S(1)} collective-permute-done((bf16[512,2,2,128]{3,2,1,0:T(2,128)(2,1)}, bf16[512,2,2,128]{3,2,1,0:T(2,128)(2,1)S(1)}, u32[]{:S(2)}, u32[]{:S(2)}) %collective-permute-start.105) | collective-permute-done | bytes 524320 | tf_op jit(solution)/shard_map/ppermute | solution.py:540
  345.2 18.0 %collective-permute-done.91.refs_1_ = bf16[1536,2,2,128]{3,2,1,0:T(2,128)(2,1)} collective-permute-done((bf16[1536,2,2,128]{3,2,1,0:T(2,128)(2,1)}, bf16[1536,2,2,128]{3,2,1,0:T(2,128)(2,1)}, u32[]{:S(2)}, u32[]{:S(2)}) %collective-permute-start.91) | collective-permute-done | bytes 1572896 | tf_op jit(solution)/shard_map/ppermute | solution.py:559
  368.9 33.6 %collective-permute-done.93.refs_3_ = bf16[1536,2,2,128]{3,2,1,0:T(2,128)(2,1)} collective-permute-done((bf16[1536,2,2,128]{3,2,1,0:T(2,128)(2,1)}, bf16[1536,2,2,128]{3,2,1,0:T(2,128)(2,1)}, u32[]{:S(2)}, u32[]{:S(2)}) %collective-permute-start.93) | collective-permute-done | bytes 1572896 | tf_op jit(solution)/shard_map/ppermute | solution.py:559
  403.0 22.3 %collective-permute-done.108.far1 = bf16[1792,2,2,128]{3,2,1,0:T(2,128)(2,1)} collective-permute-done((bf16[1792,2,2,128]{3,2,1,0:T(2,128)(2,1)}, bf16[1792,2,2,128]{3,2,1,0:T(2,128)(2,1)}, u32[]{:S(2)}, u32[]{:S(2)}) %collective-permute-start.108) | collective-permute-done | bytes 1835040 | tf_op jit(solution)/shard_map/ppermute | solution.py:540
  426.6 12.0 %fusion.12 = bf16[1,3584]{1,0:T(2,128)(2,1)} fusion(bf16[4096,1]{0,1:T(2,128)(2,1)S(1)} %bitcast.68, bf16[4096,3584]{1,0:T(8,128)(2,1)} %param.32, bf16[1,3584]{1,0:T(2,128)(2,1)} %param.27), kind=kOutput, calls=%fused_computation.13 | convolution fusion | flops 29370880 | bytes 29382656 | tf_op jit(solution)/shard_map/dot_general | solution.py:615
  443.3 7.3 %shard_map.122.refs_8_ = bf16[4096,2,4,2,128]{4,3,2,1,0:T(2,128)(2,1)} custom-call(s32[4]{0:T(128)} %lens_ref.29, bf16[2,4,2,128]{3,2,1,0:T(2,128)(2,1)} %bitcast.70, bf16[4096,2,2,128]{3,2,1,0:T(2,128)(2,1)} %get-tuple-element.561.own, bf16[4096,2,2,128]{3,2,1,0:T(2,128)(2,1)} %collective-permute-done.90.near, ...), custom_call_target="tpu_custom_call", output_to_operand_aliasing={{}: (6, {})} | custom-call | flops 1000000000 | bytes 16777216 | tf_op jit(solution)/shard_map/pallas_call | solution.py:471
  450.6 6.9 %shard_map.125.refs_0_ = bf16[4096,2,4,2,128]{4,3,2,1,0:T(2,128)(2,1)} custom-call(s32[4]{0:T(128)} %lens_ref.29, bf16[2,4,2,128]{3,2,1,0:T(2,128)(2,1)} %bitcast.64, bf16[4096,2,2,128]{3,2,1,0:T(2,128)(2,1)} %get-tuple-element.580.own, bf16[4096,2,2,128]{3,2,1,0:T(2,128)(2,1)} %collective-permute-done.102.near, bf16[1792,2,2,128]{3,2,1,0:T(2,128)(2,1)} %copy-done, ...), custom_call_target="tpu_custom_call" | custom-call | flops 1000000000 | bytes 14680064 | tf_op jit(solution)/shard_map/pallas_call | solution.py:471
  462.8 6.6 %shard_map.123 = bf16[4096,2,4,2,128]{4,3,2,1,0:T(2,128)(2,1)} custom-call(s32[4]{0:T(128)} %lens_ref.29, bf16[2,4,2,128]{3,2,1,0:T(2,128)(2,1)} %bitcast.71, bf16[4096,2,2,128]{3,2,1,0:T(2,128)(2,1)} %get-tuple-element.561.own, bf16[4096,2,2,128]{3,2,1,0:T(2,128)(2,1)} %collective-permute-done.90.near, ...), custom_call_target="tpu_custom_call", output_to_operand_aliasing={{}: (12, {})} | custom-call | flops 1000000000 | bytes 16777216 | tf_op jit(solution)/shard_map/pallas_call | solution.py:423
  469.4 6.6 %shard_map.127.refs_0_ = bf16[4096,2,4,2,128]{4,3,2,1,0:T(2,128)(2,1)} custom-call(s32[4]{0:T(128)} %lens_ref.29, bf16[2,4,2,128]{3,2,1,0:T(2,128)(2,1)} %bitcast.66, bf16[4096,2,2,128]{3,2,1,0:T(2,128)(2,1)} %get-tuple-element.580.own, bf16[4096,2,2,128]{3,2,1,0:T(2,128)(2,1)} %collective-permute-done.102.near, ...), custom_call_target="tpu_custom_call", output_to_operand_aliasing={{}: (12, {})} | custom-call | flops 1000000000 | bytes 16777216 | tf_op jit(solution)/shard_map/pallas_call | solution.py:423
  (140 shorter events, 77.7 us)
Async XLA Ops:
  7.7 91.6 %collective-permute-start.87 = (bf16[1536,2,2,128]{3,2,1,0:T(2,128)(2,1)}, bf16[1536,2,2,128]{3,2,1,0:T(2,128)(2,1)}, u32[]{:S(2)}, u32[]{:S(2)}) collective-permute-start(bf16[1536,2,2,128]{3,2,1,0:T(2,128)(2,1)} %get-tuple-element.526), channel_id=1, source_target_pairs={{0,4},{4,0},{8,12},{12,8},{1,5},{5,1},{9,13},{13,9},{2,6},{6,2},{1... | collective-permute-start | bytes 4718600 | tf_op jit(solution)/shard_map/ppermute | solution.py:559
  13.0 86.4 %collective-permute-start.88 = (bf16[1536,2,2,128]{3,2,1,0:T(2,128)(2,1)}, bf16[1536,2,2,128]{3,2,1,0:T(2,128)(2,1)}, u32[]{:S(2)}, u32[]{:S(2)}) collective-permute-start(bf16[1536,2,2,128]{3,2,1,0:T(2,128)(2,1)} %get-tuple-element.527), channel_id=1, source_target_pairs={{0,8},{4,12},{8,0},{12,4},{1,9},{5,13},{9,1},{13,5},{2,10},{6,14},... | collective-permute-start | bytes 4718600 | tf_op jit(solution)/shard_map/ppermute | solution.py:559
  13.0 86.4 %collective-permute-start.89 = (bf16[1536,2,2,128]{3,2,1,0:T(2,128)(2,1)}, bf16[1536,2,2,128]{3,2,1,0:T(2,128)(2,1)}, u32[]{:S(2)}, u32[]{:S(2)}) collective-permute-start(bf16[1536,2,2,128]{3,2,1,0:T(2,128)(2,1)} %get-tuple-element.528), channel_id=1, source_target_pairs={{0,12},{4,8},{8,4},{12,0},{1,13},{5,9},{9,5},{13,1},{2,14},{6,10},... | collective-permute-start | bytes 4718600 | tf_op jit(solution)/shard_map/ppermute | solution.py:559
  14.5 66.8 %collective-permute-start.86 = (s32[4]{0:T(128)}, s32[4]{0:T(128)}, u32[]{:S(2)}, u32[]{:S(2)}) collective-permute-start(s32[4]{0:T(128)} %lens_ref.29), channel_id=1, source_target_pairs={{0,12},{4,8},{8,4},{12,0},{1,13},{5,9},{9,5},{13,1},{2,14},{6,10},... | collective-permute-start | bytes 56 | tf_op jit(solution)/shard_map/ppermute | solution.py:559
  15.9 67.0 %collective-permute-start.85 = (s32[4]{0:T(128)}, s32[4]{0:T(128)}, u32[]{:S(2)}, u32[]{:S(2)}) collective-permute-start(s32[4]{0:T(128)} %lens_ref.29), channel_id=1, source_target_pairs={{0,8},{4,12},{8,0},{12,4},{1,9},{5,13},{9,1},{13,5},{2,10},{6,14},... | collective-permute-start | bytes 56 | tf_op jit(solution)/shard_map/ppermute | solution.py:559
  104.4 15.0 %collective-permute-start.28 = (bf16[512,2,2,128]{3,2,1,0:T(2,128)(2,1)}, bf16[512,2,2,128]{3,2,1,0:T(2,128)(2,1)S(1)}, u32[]{:S(2)}, u32[]{:S(2)}) collective-permute-start(bf16[512,2,2,128]{3,2,1,0:T(2,128)(2,1)} %get-tuple-element.397), channel_id=1, source_target_pairs={{0,2},{1,3},{2,0},{3,1},{4,6},{5,7},{6,4},{7,5},{8,10},{9,11},{10,... | collective-permute-start | bytes 1572872 | tf_op jit(solution)/shard_map/cond/branch_8_fun/ppermute | solution.py:598
  104.6 26.0 %collective-permute-start.29 = (bf16[512,2,2,128]{3,2,1,0:T(2,128)(2,1)}, bf16[512,2,2,128]{3,2,1,0:T(2,128)(2,1)S(1)}, u32[]{:S(2)}, u32[]{:S(2)}) collective-permute-start(bf16[512,2,2,128]{3,2,1,0:T(2,128)(2,1)} %get-tuple-element.398), channel_id=1, source_target_pairs={{0,2},{1,3},{2,0},{3,1},{4,6},{5,7},{6,4},{7,5},{8,10},{9,11},{10,... | collective-permute-start | bytes 1572872 | tf_op jit(solution)/shard_map/cond/branch_8_fun/ppermute | solution.py:598
  106.4 35.4 %collective-permute-start.30 = (bf16[512,2,2,128]{3,2,1,0:T(2,128)(2,1)}, bf16[512,2,2,128]{3,2,1,0:T(2,128)(2,1)S(1)}, u32[]{:S(2)}, u32[]{:S(2)}) collective-permute-start(bf16[512,2,2,128]{3,2,1,0:T(2,128)(2,1)} %get-tuple-element.399), channel_id=1, source_target_pairs={{0,2},{1,3},{2,0},{3,1},{4,6},{5,7},{6,4},{7,5},{8,10},{9,11},{10,... | collective-permute-start | bytes 1572872 | tf_op jit(solution)/shard_map/cond/branch_8_fun/ppermute | solution.py:598
  106.7 46.4 %collective-permute-start.31 = (bf16[512,2,2,128]{3,2,1,0:T(2,128)(2,1)}, bf16[512,2,2,128]{3,2,1,0:T(2,128)(2,1)S(1)}, u32[]{:S(2)}, u32[]{:S(2)}) collective-permute-start(bf16[512,2,2,128]{3,2,1,0:T(2,128)(2,1)} %get-tuple-element.400), channel_id=1, source_target_pairs={{0,2},{1,3},{2,0},{3,1},{4,6},{5,7},{6,4},{7,5},{8,10},{9,11},{10,... | collective-permute-start | bytes 1572872 | tf_op jit(solution)/shard_map/cond/branch_8_fun/ppermute | solution.py:598
  108.4 55.9 %collective-permute-start.32 = (bf16[512,2,2,128]{3,2,1,0:T(2,128)(2,1)}, bf16[512,2,2,128]{3,2,1,0:T(2,128)(2,1)S(1)}, u32[]{:S(2)}, u32[]{:S(2)}) collective-permute-start(bf16[512,2,2,128]{3,2,1,0:T(2,128)(2,1)} %get-tuple-element.401), channel_id=1, source_target_pairs={{0,2},{1,3},{2,0},{3,1},{4,6},{5,7},{6,4},{7,5},{8,10},{9,11},{10,... | collective-permute-start | bytes 1572872 | tf_op jit(solution)/shard_map/cond/branch_8_fun/ppermute | solution.py:598
  119.4 56.2 %collective-permute-start.33 = (bf16[512,2,2,128]{3,2,1,0:T(2,128)(2,1)}, bf16[512,2,2,128]{3,2,1,0:T(2,128)(2,1)S(1)}, u32[]{:S(2)}, u32[]{:S(2)}) collective-permute-start(bf16[512,2,2,128]{3,2,1,0:T(2,128)(2,1)} %get-tuple-element.402), channel_id=1, source_target_pairs={{0,2},{1,3},{2,0},{3,1},{4,6},{5,7},{6,4},{7,5},{8,10},{9,11},{10,... | collective-permute-start | bytes 1572872 | tf_op jit(solution)/shard_map/cond/branch_8_fun/ppermute | solution.py:598
  130.6 56.2 %collective-permute-start.34 = (bf16[512,2,2,128]{3,2,1,0:T(2,128)(2,1)}, bf16[512,2,2,128]{3,2,1,0:T(2,128)(2,1)S(1)}, u32[]{:S(2)}, u32[]{:S(2)}) collective-permute-start(bf16[512,2,2,128]{3,2,1,0:T(2,128)(2,1)} %get-tuple-element.403), channel_id=1, source_target_pairs={{0,2},{1,3},{2,0},{3,1},{4,6},{5,7},{6,4},{7,5},{8,10},{9,11},{10,... | collective-permute-start | bytes 1572872 | tf_op jit(solution)/shard_map/cond/branch_8_fun/ppermute | solution.py:598
  141.9 53.2 %collective-permute-start.35 = (bf16[512,2,2,128]{3,2,1,0:T(2,128)(2,1)}, bf16[512,2,2,128]{3,2,1,0:T(2,128)(2,1)S(1)}, u32[]{:S(2)}, u32[]{:S(2)}) collective-permute-start(bf16[512,2,2,128]{3,2,1,0:T(2,128)(2,1)} %get-tuple-element.404), channel_id=1, source_target_pairs={{0,2},{1,3},{2,0},{3,1},{4,6},{5,7},{6,4},{7,5},{8,10},{9,11},{10,... | collective-permute-start | bytes 1572872 | tf_op jit(solution)/shard_map/cond/branch_8_fun/ppermute | solution.py:598
  197.8 129.9 %collective-permute-start.98 = (bf16[2048,2,2,128]{3,2,1,0:T(2,128)(2,1)}, bf16[2048,2,2,128]{3,2,1,0:T(2,128)(2,1)}, u32[]{:S(2)}, u32[]{:S(2)}) collective-permute-start(bf16[2048,2,2,128]{3,2,1,0:T(2,128)(2,1)} %get-tuple-element.541._), channel_id=1, source_target_pairs={{0,2},{1,3},{2,0},{3,1},{4,6},{5,7},{6,4},{7,5},{8,10},{9,11},{10,... | collective-permute-start | bytes 6291464 | tf_op jit(solution)/shard_map/ppermute | solution.py:540
  198.0 114.1 %collective-permute-start.100 = (bf16[512,2,2,128]{3,2,1,0:T(2,128)(2,1)}, bf16[512,2,2,128]{3,2,1,0:T(2,128)(2,1)}, u32[]{:S(2)}, u32[]{:S(2)}) collective-permute-start(bf16[512,2,2,128]{3,2,1,0:T(2,128)(2,1)} %get-tuple-element.524._), channel_id=1, source_target_pairs={{0,2},{1,3},{2,0},{3,1},{4,6},{5,7},{6,4},{7,5},{8,10},{9,11},{10,... | collective-permute-start | bytes 1572872 | tf_op jit(solution)/shard_map/ppermute | solution.py:540
  200.2 129.3 %collective-permute-start.99 = (bf16[2048,2,2,128]{3,2,1,0:T(2,128)(2,1)}, bf16[2048,2,2,128]{3,2,1,0:T(2,128)(2,1)}, u32[]{:S(2)}, u32[]{:S(2)}) collective-permute-start(bf16[2048,2,2,128]{3,2,1,0:T(2,128)(2,1)} %get-tuple-element.578), channel_id=1, source_target_pairs={{0,3},{1,2},{2,1},{3,0},{4,7},{5,6},{6,5},{7,4},{8,11},{9,10},{10,... | collective-permute-start | bytes 6291464 | tf_op jit(solution)/shard_map/ppermute | solution.py:540
  244.9 56.1 %collective-permute-start.83 = (bf16[1,2048]{1,0:T(2,128)(2,1)}, bf16[1,2048]{1,0:T(2,128)(2,1)}, u32[]{:S(2)}, u32[]{:S(2)}) collective-permute-start(bf16[1,2048]{1,0:T(2,128)(2,1)} %get-tuple-element.591), channel_id=1, source_target_pairs={{0,3},{1,2},{2,1},{3,0},{4,7},{5,6},{6,5},{7,4},{8,11},{9,10},{10,... | collective-permute-start | bytes 12296 | tf_op jit(solution)/shard_map/ppermute | solution.py:540
  246.6 64.9 %collective-permute-start.82 = (bf16[1,2048]{1,0:T(2,128)(2,1)}, bf16[1,2048]{1,0:T(2,128)(2,1)}, u32[]{:S(2)}, u32[]{:S(2)}) collective-permute-start(bf16[1,2048]{1,0:T(2,128)(2,1)} %get-tuple-element.592), channel_id=1, source_target_pairs={{0,2},{1,3},{2,0},{3,1},{4,6},{5,7},{6,4},{7,5},{8,10},{9,11},{10,... | collective-permute-start | bytes 12296 | tf_op jit(solution)/shard_map/ppermute | solution.py:540
  311.6 114.5 %collective-permute-start.90 = (bf16[4096,2,2,128]{3,2,1,0:T(2,128)(2,1)}, bf16[4096,2,2,128]{3,2,1,0:T(2,128)(2,1)}, u32[]{:S(2)}, u32[]{:S(2)}) collective-permute-start(bf16[4096,2,2,128]{3,2,1,0:T(2,128)(2,1)} %get-tuple-element.562), channel_id=1, source_target_pairs={{0,1},{1,0},{2,3},{3,2},{4,5},{5,4},{6,7},{7,6},{8,9},{9,8},{10,11... | collective-permute-start | bytes 12582920 | tf_op jit(solution)/shard_map/ppermute | solution.py:540
  311.6 114.5 %collective-permute-start.102 = (bf16[4096,2,2,128]{3,2,1,0:T(2,128)(2,1)}, bf16[4096,2,2,128]{3,2,1,0:T(2,128)(2,1)}, u32[]{:S(2)}, u32[]{:S(2)}) collective-permute-start(bf16[4096,2,2,128]{3,2,1,0:T(2,128)(2,1)} %get-tuple-element.581), channel_id=1, source_target_pairs={{0,1},{1,0},{2,3},{3,2},{4,5},{5,4},{6,7},{7,6},{8,9},{9,8},{10,11... | collective-permute-start | bytes 12582920 | tf_op jit(solution)/shard_map/ppermute | solution.py:540
  326.4 36.8 %collective-permute-start.91 = (bf16[1536,2,2,128]{3,2,1,0:T(2,128)(2,1)}, bf16[1536,2,2,128]{3,2,1,0:T(2,128)(2,1)}, u32[]{:S(2)}, u32[]{:S(2)}) collective-permute-start(bf16[1536,2,2,128]{3,2,1,0:T(2,128)(2,1)} %get-tuple-element.575), channel_id=1, source_target_pairs={{0,4},{4,0},{8,12},{12,8},{1,5},{5,1},{9,13},{13,9},{2,6},{6,2},{1... | collective-permute-start | bytes 4718600 | tf_op jit(solution)/shard_map/ppermute | solution.py:559
  327.6 36.6 %collective-permute-start.92 = (bf16[1536,2,2,128]{3,2,1,0:T(2,128)(2,1)}, bf16[1536,2,2,128]{3,2,1,0:T(2,128)(2,1)}, u32[]{:S(2)}, u32[]{:S(2)}) collective-permute-start(bf16[1536,2,2,128]{3,2,1,0:T(2,128)(2,1)} %get-tuple-element.576), channel_id=1, source_target_pairs={{0,8},{4,12},{8,0},{12,4},{1,9},{5,13},{9,1},{13,5},{2,10},{6,14},... | collective-permute-start | bytes 4718600 | tf_op jit(solution)/shard_map/ppermute | solution.py:559
  343.5 59.2 %collective-permute-start.107 = (bf16[1792,2,2,128]{3,2,1,0:T(2,128)(2,1)}, bf16[1792,2,2,128]{3,2,1,0:T(2,128)(2,1)S(1)}, u32[]{:S(2)}, u32[]{:S(2)}) collective-permute-start(bf16[1792,2,2,128]{3,2,1,0:T(2,128)(2,1)} %get-tuple-element.586._), channel_id=1, source_target_pairs={{0,2},{1,3},{2,0},{3,1},{4,6},{5,7},{6,4},{7,5},{8,10},{9,11},{10,... | collective-permute-start | bytes 5505032 | tf_op jit(solution)/shard_map/ppermute | solution.py:540
  363.2 62.0 %collective-permute-start.108 = (bf16[1792,2,2,128]{3,2,1,0:T(2,128)(2,1)}, bf16[1792,2,2,128]{3,2,1,0:T(2,128)(2,1)}, u32[]{:S(2)}, u32[]{:S(2)}) collective-permute-start(bf16[1792,2,2,128]{3,2,1,0:T(2,128)(2,1)} %get-tuple-element.587), channel_id=1, source_target_pairs={{0,3},{1,2},{2,1},{3,0},{4,7},{5,6},{6,5},{7,4},{8,11},{9,10},{10,... | collective-permute-start | bytes 5505032 | tf_op jit(solution)/shard_map/ppermute | solution.py:540
  364.3 38.3 %collective-permute-start.93 = (bf16[1536,2,2,128]{3,2,1,0:T(2,128)(2,1)}, bf16[1536,2,2,128]{3,2,1,0:T(2,128)(2,1)}, u32[]{:S(2)}, u32[]{:S(2)}) collective-permute-start(bf16[1536,2,2,128]{3,2,1,0:T(2,128)(2,1)} %get-tuple-element.577), channel_id=1, source_target_pairs={{0,12},{4,8},{8,4},{12,0},{1,13},{5,9},{9,5},{13,1},{2,14},{6,10},... | collective-permute-start | bytes 4718600 | tf_op jit(solution)/shard_map/ppermute | solution.py:559
  402.5 56.7 %collective-permute-start.94 = (bf16[1536,2,2,128]{3,2,1,0:T(2,128)(2,1)}, bf16[1536,2,2,128]{3,2,1,0:T(2,128)(2,1)}, u32[]{:S(2)}, u32[]{:S(2)}) collective-permute-start(bf16[1536,2,2,128]{3,2,1,0:T(2,128)(2,1)} %get-tuple-element.574.refs_0_), channel_id=1, source_target_pairs={{0,1},{1,0},{2,3},{3,2},{4,5},{5,4},{6,7},{7,6},{8,9},{9,8},{10,11... | collective-permute-start | bytes 4718600 | tf_op jit(solution)/shard_map/ppermute | solution.py:540
  402.6 54.9 %collective-permute-start.106 = (bf16[512,2,2,128]{3,2,1,0:T(2,128)(2,1)}, bf16[512,2,2,128]{3,2,1,0:T(2,128)(2,1)}, u32[]{:S(2)}, u32[]{:S(2)}) collective-permute-start(bf16[512,2,2,128]{3,2,1,0:T(2,128)(2,1)} %get-tuple-element.585), channel_id=1, source_target_pairs={{0,3},{1,2},{2,1},{3,0},{4,7},{5,6},{6,5},{7,4},{8,11},{9,10},{10,... | collective-permute-start | bytes 1572872 | tf_op jit(solution)/shard_map/ppermute | solution.py:540
  425.3 37.5 %collective-permute-start.95 = (bf16[1536,2,2,128]{3,2,1,0:T(2,128)(2,1)}, bf16[1536,2,2,128]{3,2,1,0:T(2,128)(2,1)}, u32[]{:S(2)}, u32[]{:S(2)}) collective-permute-start(bf16[1536,2,2,128]{3,2,1,0:T(2,128)(2,1)} %collective-permute-done.91.refs_1_), channel_id=1, source_target_pairs={{0,1},{1,0},{2,3},{3,2},{4,5},{5,4},{6,7},{7,6},{8,9},{9,8},{10,11... | collective-permute-start | bytes 4718600 | tf_op jit(solution)/shard_map/ppermute | solution.py:540
  426.1 36.6 %collective-permute-start.96 = (bf16[1536,2,2,128]{3,2,1,0:T(2,128)(2,1)}, bf16[1536,2,2,128]{3,2,1,0:T(2,128)(2,1)}, u32[]{:S(2)}, u32[]{:S(2)}) collective-permute-start(bf16[1536,2,2,128]{3,2,1,0:T(2,128)(2,1)} %collective-permute-done.92.refs_2_), channel_id=1, source_target_pairs={{0,1},{1,0},{2,3},{3,2},{4,5},{5,4},{6,7},{7,6},{8,9},{9,8},{10,11... | collective-permute-start | bytes 4718600 | tf_op jit(solution)/shard_map/ppermute | solution.py:540
  426.1 36.6 %collective-permute-start.97 = (bf16[1536,2,2,128]{3,2,1,0:T(2,128)(2,1)}, bf16[1536,2,2,128]{3,2,1,0:T(2,128)(2,1)}, u32[]{:S(2)}, u32[]{:S(2)}) collective-permute-start(bf16[1536,2,2,128]{3,2,1,0:T(2,128)(2,1)} %collective-permute-done.93.refs_3_), channel_id=1, source_target_pairs={{0,1},{1,0},{2,3},{3,2},{4,5},{5,4},{6,7},{7,6},{8,9},{9,8},{10,11... | collective-permute-start | bytes 4718600 | tf_op jit(solution)/shard_map/ppermute | solution.py:540
  457.6 18.4 %collective-permute-start.103 = (bf16[256,2,2,128]{3,2,1,0:T(2,128)(2,1)}, bf16[256,2,2,128]{3,2,1,0:T(2,128)(2,1)}, u32[]{:S(2)}, u32[]{:S(2)}) collective-permute-start(bf16[256,2,2,128]{3,2,1,0:T(2,128)(2,1)} %get-tuple-element.582), channel_id=1, source_target_pairs={{0,2},{1,3},{2,0},{3,1},{4,6},{5,7},{6,4},{7,5},{8,10},{9,11},{10,... | collective-permute-start | bytes 786440 | tf_op jit(solution)/shard_map/ppermute | solution.py:540
  459.3 16.7 %collective-permute-start.104 = (bf16[256,2,2,128]{3,2,1,0:T(2,128)(2,1)}, bf16[256,2,2,128]{3,2,1,0:T(2,128)(2,1)}, u32[]{:S(2)}, u32[]{:S(2)}) collective-permute-start(bf16[256,2,2,128]{3,2,1,0:T(2,128)(2,1)} %get-tuple-element.583), channel_id=1, source_target_pairs={{0,3},{1,2},{2,1},{3,0},{4,7},{5,6},{6,5},{7,4},{8,11},{9,10},{10,... | collective-permute-start | bytes 786440 | tf_op jit(solution)/shard_map/ppermute | solution.py:540
  (14 other events, 485.1 us)
where the time goes:
time: 481 us; the launch traced here: 479 us
  waiting for transfers between devices  268 us (56%)
  Pallas kernels  90 us (19%)
  matrix products  53.7 us (11%)
  starting transfers between devices  39.3 us (8%)
  between operations  13 us (3%)
  local copies, waits for them, and re-layouts  12.1 us (3%)
    ppermute x9, waiting for transfers between devices, shift(): return lax.ppermute(array, 'dp', [(g, g ^ d) for g in range(LANES_OF_CUT)])  101 us
    ppermute x22, waiting for transfers between devices, swap(): return lax.ppermute(array, 'sh', [(i, i ^ j) for i in range(group)])  86.7 us
    ppermute x8, waiting for transfers between devices, branch(): lax.ppermute(a, 'sh', [(i, i ^ 2) for i in range(group)])  80.1 us
    pallas_call x7, Pallas kernels, build(): pl.pallas_call(functools.partial(build_kernel, partners, c0), out_shape=[...  39.2 us
    pallas_call x5, Pallas kernels, local_call(): pl.pallas_call(kernel, out_shape=outs, in_specs=[pl.BlockSpec(memory_spac...  26.5 us
    pallas_call x5, Pallas kernels, place(): pl.pallas_call(functools.partial(place_kernel, c0, size, prev is not None...  24.3 us
    dot_general x1, matrix products, attend_heads(): jnp.einsum('rkgd,rwkd->rkgw', q_heads, k_prefill, preferred_element_type=...  18.9 us
    ppermute x22, starting transfers between devices, swap(): return lax.ppermute(array, 'sh', [(i, i ^ j) for i in range(group)])  17.7 us
  transfers between devices with their start and end apart: 39, of which 18 were waited for; matrix products, arithmetic and copies ran while one was open for 14% of the time, Pallas kernels for 16%

commit v1 on v0

--- a/solution.py
+++ b/solution.py
@@ -24,7 +24,7 @@
 UNIT = 128
 UPPER = (WINDOW - LOW) // UNIT
 LANES_OF_CUT = 4
-PART = 4
+PART = 3
 
 
 def build_kernel(partners, c0, lens_ref, src_ref, _, *refs):
@@ -207,7 +207,7 @@
 
 
 def used_units(length):
-    return (jnp.maximum(jnp.minimum(length, WINDOW) - LOW, 0) + UNIT - 1) // UNIT
+    return (jnp.maximum(jnp.minimum(length, WINDOW) - LOW, 0) + UNIT - 1) >> 7
 
 
 def lane_counts(lens, half, lane):
@@ -588,10 +588,9 @@
         parts = compact(every_length, dealt, False)
         parts, v_built = lax.optimization_barrier((parts, v_built))
         by_group = every_length.reshape(LANES_OF_CUT, group)
-        level = jnp.int32(0)
-        for half in range(2):
-            for lane in range(LANES_OF_CUT):
-                level = jnp.maximum(level, sum(lane_counts(lambda g, row: by_group[g, row], half, lane)))
+        totals = used_units(by_group).reshape(LANES_OF_CUT, 2, 2).sum(-1) * 2
+        lanes = jnp.arange(LANES_OF_CUT, dtype=jnp.int32)
+        level = jnp.max(jnp.sum(jnp.right_shift(totals[:, :, None] + (LANES_OF_CUT - 1 - lanes), 2), axis=0))
 
         def cross(count):
             def branch(*arrays):
@@ -599,7 +598,7 @@
 
             return branch
 
-        parts = lax.switch((level + PART - 1) // PART, [cross(count) for count in range(len(parts) + 1)], *parts)
+        parts = lax.switch(lax.div(level + PART - 1, PART), [cross(count) for count in range(len(parts) + 1)], *parts)
 
         v_far = [send_far(built) for built in v_built]
         dealt = compact(every_length, parts, True)
@@ -622,7 +621,7 @@
             fresh = fresh.reshape(fresh.shape[0], group, kv_heads, LANES)
             out, c0 = None, 0
             for far0, far1 in far:
-                if values and c0 + far0.shape[0] == LOW:
+                if values and c0 == V_CHUNKS[0]:
                     out = place_upper(values, lengths, fresh, own, near, dealt, others, out)
                 out = place(lengths, fresh, own, near, far0, far1, c0, out)
                 c0 += far0.shape[0]

time: 481 us -> 508 us (1.056)
  waiting for transfers between devices: 268 us -> 307 us
  between operations: 13 us -> 1.99 us
    ppermute x22, waiting for transfers between devices: 86.7 us -> 128 us  [swap(): return lax.ppermute(array, 'sh', [(i, i ^ j) for i in range(group)])]
    ppermute x8 -> x10, waiting for transfers between devices: 80.1 us -> 74.6 us  [branch(): lax.ppermute(a, 'sh', [(i, i ^ 2) for i in range(group)])]
  transfers between devices with their start and end apart: 39 -> 41, of which waited for: 18 -> 20; matrix products, arithmetic and copies ran while one was open for 14% -> 14% of each run, Pallas kernels for 16% -> 16%
where the time goes in v1:
time: 508 us; the launch traced here: 506 us
  waiting for transfers between devices  307 us (60%)
  Pallas kernels  90.1 us (18%)
  matrix products  53.5 us (11%)
  starting transfers between devices  37 us (7%)
  local copies, waits for them, and re-layouts  12.7 us (2%)
    ppermute x22, waiting for transfers between devices, swap(): return lax.ppermute(array, 'sh', [(i, i ^ j) for i in range(group)])  128 us
    ppermute x9, waiting for transfers between devices, shift(): return lax.ppermute(array, 'dp', [(g, g ^ d) for g in range(LANES_OF_CUT)])  105 us
    ppermute x10, waiting for transfers between devices, branch(): lax.ppermute(a, 'sh', [(i, i ^ 2) for i in range(group)])  74.6 us
    pallas_call x7, Pallas kernels, build(): pl.pallas_call(functools.partial(build_kernel, partners, c0), out_shape=[...  39.3 us
    pallas_call x5, Pallas kernels, local_call(): pl.pallas_call(kernel, out_shape=outs, in_specs=[pl.BlockSpec(memory_spac...  26.5 us
    pallas_call x5, Pallas kernels, place(): pl.pallas_call(functools.partial(place_kernel, c0, size, prev is not None...  24.3 us
    dot_general x1, matrix products, attend_heads(): jnp.einsum('rkgd,rwkd->rkgw', q_heads, k_prefill, preferred_element_type=...  18.7 us
    ppermute x22, starting transfers between devices, swap(): return lax.ppermute(array, 'sh', [(i, i ^ j) for i in range(group)])  17.2 us
  transfers between devices with their start and end apart: 41, of which 20 were waited for; matrix products, arithmetic and copies ran while one was open for 14% of the time, Pallas kernels for 16%

profile of v1, /device:TPU:0, one launch (start us, length us, event | category | flops | bytes accessed | tf_op | source)
XLA Modules:
  0.0 506.5 jit_solution(17936448245780468800)
XLA Ops:
  0.6 4.3 collective-permute-start.144
  16.2 5.7 %shard_map.115 = (bf16[2048,2,2,128]{3,2,1,0:T(2,128)(2,1)}, bf16[2048,2,2,128]{3,2,1,0:T(2,128)(2,1)}) custom-call(s32[4]{0:T(128)} %lens_ref.29, bf16[4,7168,2,2,128]{4,3,2,1,0:T(2,128)(2,1)} %bitcast.44, bf16[1536,2,2,128]{3,2,1,0:T(2,128)(2,1)} %get-tuple-element.881.refs_0_._), custom_call_target="tpu_custom_call" | custom-call | flops 1000000000 | bytes 8388608 | tf_op jit(solution)/shard_map/pallas_call | solution.py:106
  26.0 4.4 shard_map.117
  36.2 46.6 %collective-permute-done.142 = s32[4]{0:T(128)S(1)} collective-permute-done((s32[4]{0:T(128)}, s32[4]{0:T(128)S(1)}, u32[]{:S(2)}, u32[]{:S(2)}) %collective-permute-start.142) | collective-permute-done | bytes 48 | tf_op jit(solution)/shard_map/ppermute | solution.py:559
  86.2 4.9 shard_map.114
  91.2 87.0 %conditional.1 = ((bf16[384,2,2,128]{3,2,1,0:T(2,128)(2,1)}, bf16[384,2,2,128]{3,2,1,0:T(2,128)(2,1)}, bf16[384,2,2,128]{3,2,1,0:T(2,128)(2,1)}, bf16[384,2,2,12...) conditional(s32[]{:T(128)} %clamp.3, ...), branch_computations={%region_7.9_spmd, %region_8.10_spmd, %region_9.11_spmd, %region_10... | conditional | bytes 37749512 | solution.py:601
  95.4 8.0 %collective-permute-done.45 = bf16[384,2,2,128]{3,2,1,0:T(2,128)(2,1)S(1)} collective-permute-done((bf16[384,2,2,128]{3,2,1,0:T(2,128)(2,1)}, bf16[384,2,2,128]{3,2,1,0:T(2,128)(2,1)S(1)}, u32[]{:S(2)}, u32[]{:S(2)}) %collective-permute-start.45) | collective-permute-done | bytes 393248 | tf_op jit(solution)/shard_map/cond/branch_10_fun/ppermute | solution.py:597
  103.6 8.3 %collective-permute-done.46 = bf16[384,2,2,128]{3,2,1,0:T(2,128)(2,1)S(1)} collective-permute-done((bf16[384,2,2,128]{3,2,1,0:T(2,128)(2,1)}, bf16[384,2,2,128]{3,2,1,0:T(2,128)(2,1)S(1)}, u32[]{:S(2)}, u32[]{:S(2)}) %collective-permute-start.46) | collective-permute-done | bytes 393248 | tf_op jit(solution)/shard_map/cond/branch_10_fun/ppermute | solution.py:597
  112.0 8.3 %collective-permute-done.47 = bf16[384,2,2,128]{3,2,1,0:T(2,128)(2,1)S(1)} collective-permute-done((bf16[384,2,2,128]{3,2,1,0:T(2,128)(2,1)}, bf16[384,2,2,128]{3,2,1,0:T(2,128)(2,1)S(1)}, u32[]{:S(2)}, u32[]{:S(2)}) %collective-permute-start.47) | collective-permute-done | bytes 393248 | tf_op jit(solution)/shard_map/cond/branch_10_fun/ppermute | solution.py:597
  120.4 8.3 %collective-permute-done.48 = bf16[384,2,2,128]{3,2,1,0:T(2,128)(2,1)S(1)} collective-permute-done((bf16[384,2,2,128]{3,2,1,0:T(2,128)(2,1)}, bf16[384,2,2,128]{3,2,1,0:T(2,128)(2,1)S(1)}, u32[]{:S(2)}, u32[]{:S(2)}) %collective-permute-start.48) | collective-permute-done | bytes 393248 | tf_op jit(solution)/shard_map/cond/branch_10_fun/ppermute | solution.py:597
  128.9 8.3 %collective-permute-done.49 = bf16[384,2,2,128]{3,2,1,0:T(2,128)(2,1)S(1)} collective-permute-done((bf16[384,2,2,128]{3,2,1,0:T(2,128)(2,1)}, bf16[384,2,2,128]{3,2,1,0:T(2,128)(2,1)S(1)}, u32[]{:S(2)}, u32[]{:S(2)}) %collective-permute-start.49) | collective-permute-done | bytes 393248 | tf_op jit(solution)/shard_map/cond/branch_10_fun/ppermute | solution.py:597
  141.1 4.6 collective-permute-done.50
  146.4 7.7 %collective-permute-done.51 = bf16[384,2,2,128]{3,2,1,0:T(2,128)(2,1)S(1)} collective-permute-done((bf16[384,2,2,128]{3,2,1,0:T(2,128)(2,1)}, bf16[384,2,2,128]{3,2,1,0:T(2,128)(2,1)S(1)}, u32[]{:S(2)}, u32[]{:S(2)}) %collective-permute-start.51) | collective-permute-done | bytes 393248 | tf_op jit(solution)/shard_map/cond/branch_10_fun/ppermute | solution.py:597
  154.8 7.7 %collective-permute-done.52 = bf16[384,2,2,128]{3,2,1,0:T(2,128)(2,1)S(1)} collective-permute-done((bf16[384,2,2,128]{3,2,1,0:T(2,128)(2,1)}, bf16[384,2,2,128]{3,2,1,0:T(2,128)(2,1)S(1)}, u32[]{:S(2)}, u32[]{:S(2)}) %collective-permute-start.52) | collective-permute-done | bytes 393248 | tf_op jit(solution)/shard_map/cond/branch_10_fun/ppermute | solution.py:597
  163.2 7.7 %collective-permute-done.53 = bf16[384,2,2,128]{3,2,1,0:T(2,128)(2,1)S(1)} collective-permute-done((bf16[384,2,2,128]{3,2,1,0:T(2,128)(2,1)}, bf16[384,2,2,128]{3,2,1,0:T(2,128)(2,1)S(1)}, u32[]{:S(2)}, u32[]{:S(2)}) %collective-permute-start.53) | collective-permute-done | bytes 393248 | tf_op jit(solution)/shard_map/cond/branch_10_fun/ppermute | solution.py:597
  171.6 5.8 %collective-permute-done.54 = bf16[384,2,2,128]{3,2,1,0:T(2,128)(2,1)S(1)} collective-permute-done((bf16[384,2,2,128]{3,2,1,0:T(2,128)(2,1)}, bf16[384,2,2,128]{3,2,1,0:T(2,128)(2,1)S(1)}, u32[]{:S(2)}, u32[]{:S(2)}) %collective-permute-start.54) | collective-permute-done | bytes 393248 | tf_op jit(solution)/shard_map/cond/branch_10_fun/ppermute | solution.py:597
  194.8 18.7 %fusion.59 = (f32[4,2,2]{2,1,0:T(2,128)S(1)}, f32[4,2,2,7168]{3,2,1,0:T(2,128)S(1)}) fusion(bf16[4,7168,2,256]{3,2,1,0:T(2,128)(2,1)} %param.28, bf16[4,2,2,128]{3,2,1,0:T(2,128)(2,1)S(1)} %get-tuple-element.965, bf16[4,2,2,128]{3,2,1,0:T(2,128)(2,1)S(1)} %get-tuple-element.964, pred[4,7168]{1,0:T(4,128)(4,1)S(1)} %fusion.35), kind=kOutput, calls=%fused_computation.94 | convolution fusion | flops 59080688 | bytes 29855808 | tf_op jit(solution)/shard_map/rkgd,rwkd->rkgw/dot_general | solution.py:519
  214.1 13.3 %fusion.20 = bf16[4,2,2,256]{3,2,1,0:T(2,128)(2,1)S(1)} fusion(bf16[4,7168,2,256]{3,2,1,0:T(2,128)(2,1)} %param.29, f32[4,2,2,7168]{3,2,1,0:T(2,128)S(1)} %get-tuple-element.975, f32[4,2,2]{2,1,0:T(2,128)S(1)} %get-tuple-element.963, f32[4,2,2]{2,1,0:T(2,128)S(1)} %multiply_maximum_fusion, f32[4,2,256]{2,1,0:T(2,128)S(1)} %reshape.338, ...), kind=kOutput, calls=%fused_computation.19 | convolution fusion | flops 59076608 | bytes 29835456 | tf_op jit(solution)/shard_map/rkgw,rwkd->rkgd/dot_general | solution.py:528
  228.8 65.7 %collective-permute-done.141 = bf16[1,2048]{1,0:T(2,128)(2,1)} collective-permute-done((bf16[1,2048]{1,0:T(2,128)(2,1)S(1)}, bf16[1,2048]{1,0:T(2,128)(2,1)}, u32[]{:S(2)}, u32[]{:S(2)}) %collective-permute-start.141) | collective-permute-done | bytes 4128 | tf_op jit(solution)/shard_map/ppermute | solution.py:540
  306.1 9.9 %shard_map.119 = (bf16[4096,2,2,128]{3,2,1,0:T(2,128)(2,1)}, bf16[4096,2,2,128]{3,2,1,0:T(2,128)(2,1)}) custom-call(s32[4]{0:T(128)} %lens_ref.29, bf16[4,7168,2,2,128]{4,3,2,1,0:T(2,128)(2,1)} %bitcast.45, bf16[384,2,2,128]{3,2,1,0:T(2,128)(2,1)} %get-tuple-element.924._.refs_0_), custom_call_target="tpu_custom_call" | custom-call | flops 1000000000 | bytes 16777216 | tf_op jit(solution)/shard_map/pallas_call | solution.py:106
  316.5 23.7 %collective-permute-done.149.refs_1_ = bf16[1536,2,2,128]{3,2,1,0:T(2,128)(2,1)} collective-permute-done((bf16[1536,2,2,128]{3,2,1,0:T(2,128)(2,1)}, bf16[1536,2,2,128]{3,2,1,0:T(2,128)(2,1)}, u32[]{:S(2)}, u32[]{:S(2)}) %collective-permute-start.149) | collective-permute-done | bytes 1572896 | tf_op jit(solution)/shard_map/ppermute | solution.py:559
  340.2 34.4 %collective-permute-done.150.refs_2_ = bf16[1536,2,2,128]{3,2,1,0:T(2,128)(2,1)} collective-permute-done((bf16[1536,2,2,128]{3,2,1,0:T(2,128)(2,1)}, bf16[1536,2,2,128]{3,2,1,0:T(2,128)(2,1)}, u32[]{:S(2)}, u32[]{:S(2)}) %collective-permute-start.150) | collective-permute-done | bytes 1572896 | tf_op jit(solution)/shard_map/ppermute | solution.py:559
  374.6 9.7 %shard_map.124 = (bf16[4096,2,2,128]{3,2,1,0:T(2,128)(2,1)}, bf16[4096,2,2,128]{3,2,1,0:T(2,128)(2,1)}) custom-call(s32[4]{0:T(128)} %lens_ref.29, bf16[4,7168,2,2,128]{4,3,2,1,0:T(2,128)(2,1)} %bitcast.41, bf16[384,2,2,128]{3,2,1,0:T(2,128)(2,1)} %get-tuple-element.924._.refs_0_), custom_call_target="tpu_custom_call" | custom-call | flops 1000000000 | bytes 16777216 | tf_op jit(solution)/shard_map/pallas_call | solution.py:106
  390.5 12.0 %fusion.12 = bf16[1,3584]{1,0:T(2,128)(2,1)} fusion(bf16[4096,1]{0,1:T(2,128)(2,1)S(1)} %bitcast.53, bf16[4096,3584]{1,0:T(8,128)(2,1)} %param.36, bf16[1,3584]{1,0:T(2,128)(2,1)} %param.31), kind=kOutput, calls=%fused_computation.13 | convolution fusion | flops 29370880 | bytes 29382656 | tf_op jit(solution)/shard_map/dot_general | solution.py:614
  409.2 7.3 %shard_map.122.refs_8_ = bf16[4096,2,4,2,128]{4,3,2,1,0:T(2,128)(2,1)} custom-call(s32[4]{0:T(128)} %lens_ref.29, bf16[2,4,2,128]{3,2,1,0:T(2,128)(2,1)} %bitcast.55, bf16[4096,2,2,128]{3,2,1,0:T(2,128)(2,1)} %get-tuple-element.925.own, bf16[4096,2,2,128]{3,2,1,0:T(2,128)(2,1)} %collective-permute-done.148.near, ...), custom_call_target="tpu_custom_call", output_to_operand_aliasing={{}: (6, {})} | custom-call | flops 1000000000 | bytes 16777216 | tf_op jit(solution)/shard_map/pallas_call | solution.py:471
  416.5 6.6 %shard_map.123 = bf16[4096,2,4,2,128]{4,3,2,1,0:T(2,128)(2,1)} custom-call(s32[4]{0:T(128)} %lens_ref.29, bf16[2,4,2,128]{3,2,1,0:T(2,128)(2,1)} %bitcast.56, bf16[4096,2,2,128]{3,2,1,0:T(2,128)(2,1)} %get-tuple-element.925.own, bf16[4096,2,2,128]{3,2,1,0:T(2,128)(2,1)} %collective-permute-done.148.near, ...), custom_call_target="tpu_custom_call", output_to_operand_aliasing={{}: (12, {})} | custom-call | flops 1000000000 | bytes 16777216 | tf_op jit(solution)/shard_map/pallas_call | solution.py:423
  423.0 8.4 %collective-permute-done.165.far0 = bf16[1792,2,2,128]{3,2,1,0:T(2,128)(2,1)} collective-permute-done((bf16[1792,2,2,128]{3,2,1,0:T(2,128)(2,1)}, bf16[1792,2,2,128]{3,2,1,0:T(2,128)(2,1)}, u32[]{:S(2)}, u32[]{:S(2)}) %collective-permute-start.165) | collective-permute-done | bytes 1835040 | tf_op jit(solution)/shard_map/ppermute | solution.py:540
  433.5 36.8 %collective-permute-done.166.far1 = bf16[1792,2,2,128]{3,2,1,0:T(2,128)(2,1)} collective-permute-done((bf16[1792,2,2,128]{3,2,1,0:T(2,128)(2,1)}, bf16[1792,2,2,128]{3,2,1,0:T(2,128)(2,1)}, u32[]{:S(2)}, u32[]{:S(2)}) %collective-permute-start.166) | collective-permute-done | bytes 1835040 | tf_op jit(solution)/shard_map/ppermute | solution.py:540
  472.3 6.9 %shard_map.125.refs_8_ = bf16[4096,2,4,2,128]{4,3,2,1,0:T(2,128)(2,1)} custom-call(s32[4]{0:T(128)} %lens_ref.29, bf16[2,4,2,128]{3,2,1,0:T(2,128)(2,1)} %bitcast.49, bf16[4096,2,2,128]{3,2,1,0:T(2,128)(2,1)} %get-tuple-element.948.own, bf16[4096,2,2,128]{3,2,1,0:T(2,128)(2,1)} %collective-permute-done.160.near, ...), custom_call_target="tpu_custom_call" | custom-call | flops 1000000000 | bytes 14680064 | tf_op jit(solution)/shard_map/pallas_call | solution.py:471
  479.2 6.6 %shard_map.126.refs_0_ = bf16[4096,2,4,2,128]{4,3,2,1,0:T(2,128)(2,1)} custom-call(s32[4]{0:T(128)} %lens_ref.29, bf16[2,4,2,128]{3,2,1,0:T(2,128)(2,1)} %bitcast.50, bf16[4096,2,2,128]{3,2,1,0:T(2,128)(2,1)} %get-tuple-element.948.own, bf16[4096,2,2,128]{3,2,1,0:T(2,128)(2,1)} %collective-permute-done.160.near, ...), custom_call_target="tpu_custom_call", output_to_operand_aliasing={{}: (12, {})} | custom-call | flops 1000000000 | bytes 16777216 | tf_op jit(solution)/shard_map/pallas_call | solution.py:423
  485.8 7.0 %collective-permute-done.164.far1 = bf16[512,2,2,128]{3,2,1,0:T(2,128)(2,1)} collective-permute-done((bf16[512,2,2,128]{3,2,1,0:T(2,128)(2,1)}, bf16[512,2,2,128]{3,2,1,0:T(2,128)(2,1)}, u32[]{:S(2)}, u32[]{:S(2)}) %collective-permute-start.164) | collective-permute-done | bytes 524320 | tf_op jit(solution)/shard_map/ppermute | solution.py:540
  498.9 4.3 collective-permute-done.162.far1
  (147 shorter events, 92.7 us)
Async XLA Ops:
  0.6 32.5 %collective-permute-start.144 = (s32[4]{0:T(128)}, s32[4]{0:T(128)}, u32[]{:S(2)}, u32[]{:S(2)}) collective-permute-start(s32[4]{0:T(128)} %lens_ref.29), channel_id=1, source_target_pairs={{0,12},{4,8},{8,4},{12,0},{1,13},{5,9},{9,5},{13,1},{2,14},{6,10},... | collective-permute-start | bytes 56 | tf_op jit(solution)/shard_map/ppermute | solution.py:559
  4.9 31.3 %collective-permute-start.143 = (s32[4]{0:T(128)}, s32[4]{0:T(128)}, u32[]{:S(2)}, u32[]{:S(2)}) collective-permute-start(s32[4]{0:T(128)} %lens_ref.29), channel_id=1, source_target_pairs={{0,8},{4,12},{8,0},{12,4},{1,9},{5,13},{9,1},{13,5},{2,10},{6,14},... | collective-permute-start | bytes 56 | tf_op jit(solution)/shard_map/ppermute | solution.py:559
  12.5 73.8 %collective-permute-start.145 = (bf16[1536,2,2,128]{3,2,1,0:T(2,128)(2,1)}, bf16[1536,2,2,128]{3,2,1,0:T(2,128)(2,1)}, u32[]{:S(2)}, u32[]{:S(2)}) collective-permute-start(bf16[1536,2,2,128]{3,2,1,0:T(2,128)(2,1)} %get-tuple-element.882), channel_id=1, source_target_pairs={{0,4},{4,0},{8,12},{12,8},{1,5},{5,1},{9,13},{13,9},{2,6},{6,2},{1... | collective-permute-start | bytes 4718600 | tf_op jit(solution)/shard_map/ppermute | solution.py:559
  14.7 71.6 %collective-permute-start.146 = (bf16[1536,2,2,128]{3,2,1,0:T(2,128)(2,1)}, bf16[1536,2,2,128]{3,2,1,0:T(2,128)(2,1)}, u32[]{:S(2)}, u32[]{:S(2)}) collective-permute-start(bf16[1536,2,2,128]{3,2,1,0:T(2,128)(2,1)} %get-tuple-element.883), channel_id=1, source_target_pairs={{0,8},{4,12},{8,0},{12,4},{1,9},{5,13},{9,1},{13,5},{2,10},{6,14},... | collective-permute-start | bytes 4718600 | tf_op jit(solution)/shard_map/ppermute | solution.py:559
  14.7 71.5 %collective-permute-start.147 = (bf16[1536,2,2,128]{3,2,1,0:T(2,128)(2,1)}, bf16[1536,2,2,128]{3,2,1,0:T(2,128)(2,1)}, u32[]{:S(2)}, u32[]{:S(2)}) collective-permute-start(bf16[1536,2,2,128]{3,2,1,0:T(2,128)(2,1)} %get-tuple-element.884), channel_id=1, source_target_pairs={{0,12},{4,8},{8,4},{12,0},{1,13},{5,9},{9,5},{13,1},{2,14},{6,10},... | collective-permute-start | bytes 4718600 | tf_op jit(solution)/shard_map/ppermute | solution.py:559
  33.1 49.6 %collective-permute-start.142 = (s32[4]{0:T(128)}, s32[4]{0:T(128)S(1)}, u32[]{:S(2)}, u32[]{:S(2)}) collective-permute-start(s32[4]{0:T(128)} %lens_ref.29), channel_id=1, source_target_pairs={{0,4},{4,0},{8,12},{12,8},{1,5},{5,1},{9,13},{13,9},{2,6},{6,2},{1... | collective-permute-start | bytes 56 | tf_op jit(solution)/shard_map/ppermute | solution.py:559
  93.3 27.0 %collective-permute-start.47 = (bf16[384,2,2,128]{3,2,1,0:T(2,128)(2,1)}, bf16[384,2,2,128]{3,2,1,0:T(2,128)(2,1)S(1)}, u32[]{:S(2)}, u32[]{:S(2)}) collective-permute-start(bf16[384,2,2,128]{3,2,1,0:T(2,128)(2,1)} %get-tuple-element.691), channel_id=1, source_target_pairs={{0,2},{1,3},{2,0},{3,1},{4,6},{5,7},{6,4},{7,5},{8,10},{9,11},{10,... | collective-permute-start | bytes 1179656 | tf_op jit(solution)/shard_map/cond/branch_10_fun/ppermute | solution.py:597
  93.4 35.3 %collective-permute-start.48 = (bf16[384,2,2,128]{3,2,1,0:T(2,128)(2,1)}, bf16[384,2,2,128]{3,2,1,0:T(2,128)(2,1)S(1)}, u32[]{:S(2)}, u32[]{:S(2)}) collective-permute-start(bf16[384,2,2,128]{3,2,1,0:T(2,128)(2,1)} %get-tuple-element.692), channel_id=1, source_target_pairs={{0,2},{1,3},{2,0},{3,1},{4,6},{5,7},{6,4},{7,5},{8,10},{9,11},{10,... | collective-permute-start | bytes 1179656 | tf_op jit(solution)/shard_map/cond/branch_10_fun/ppermute | solution.py:597
  95.3 41.8 %collective-permute-start.49 = (bf16[384,2,2,128]{3,2,1,0:T(2,128)(2,1)}, bf16[384,2,2,128]{3,2,1,0:T(2,128)(2,1)S(1)}, u32[]{:S(2)}, u32[]{:S(2)}) collective-permute-start(bf16[384,2,2,128]{3,2,1,0:T(2,128)(2,1)} %get-tuple-element.693), channel_id=1, source_target_pairs={{0,2},{1,3},{2,0},{3,1},{4,6},{5,7},{6,4},{7,5},{8,10},{9,11},{10,... | collective-permute-start | bytes 1179656 | tf_op jit(solution)/shard_map/cond/branch_10_fun/ppermute | solution.py:597
  103.5 42.1 %collective-permute-start.50 = (bf16[384,2,2,128]{3,2,1,0:T(2,128)(2,1)}, bf16[384,2,2,128]{3,2,1,0:T(2,128)(2,1)S(1)}, u32[]{:S(2)}, u32[]{:S(2)}) collective-permute-start(bf16[384,2,2,128]{3,2,1,0:T(2,128)(2,1)} %get-tuple-element.694), channel_id=1, source_target_pairs={{0,2},{1,3},{2,0},{3,1},{4,6},{5,7},{6,4},{7,5},{8,10},{9,11},{10,... | collective-permute-start | bytes 1179656 | tf_op jit(solution)/shard_map/cond/branch_10_fun/ppermute | solution.py:597
  111.9 42.1 %collective-permute-start.51 = (bf16[384,2,2,128]{3,2,1,0:T(2,128)(2,1)}, bf16[384,2,2,128]{3,2,1,0:T(2,128)(2,1)S(1)}, u32[]{:S(2)}, u32[]{:S(2)}) collective-permute-start(bf16[384,2,2,128]{3,2,1,0:T(2,128)(2,1)} %get-tuple-element.695), channel_id=1, source_target_pairs={{0,2},{1,3},{2,0},{3,1},{4,6},{5,7},{6,4},{7,5},{8,10},{9,11},{10,... | collective-permute-start | bytes 1179656 | tf_op jit(solution)/shard_map/cond/branch_10_fun/ppermute | solution.py:597
  120.3 42.1 %collective-permute-start.52 = (bf16[384,2,2,128]{3,2,1,0:T(2,128)(2,1)}, bf16[384,2,2,128]{3,2,1,0:T(2,128)(2,1)S(1)}, u32[]{:S(2)}, u32[]{:S(2)}) collective-permute-start(bf16[384,2,2,128]{3,2,1,0:T(2,128)(2,1)} %get-tuple-element.696), channel_id=1, source_target_pairs={{0,2},{1,3},{2,0},{3,1},{4,6},{5,7},{6,4},{7,5},{8,10},{9,11},{10,... | collective-permute-start | bytes 1179656 | tf_op jit(solution)/shard_map/cond/branch_10_fun/ppermute | solution.py:597
  128.8 42.1 %collective-permute-start.53 = (bf16[384,2,2,128]{3,2,1,0:T(2,128)(2,1)}, bf16[384,2,2,128]{3,2,1,0:T(2,128)(2,1)S(1)}, u32[]{:S(2)}, u32[]{:S(2)}) collective-permute-start(bf16[384,2,2,128]{3,2,1,0:T(2,128)(2,1)} %get-tuple-element.697), channel_id=1, source_target_pairs={{0,2},{1,3},{2,0},{3,1},{4,6},{5,7},{6,4},{7,5},{8,10},{9,11},{10,... | collective-permute-start | bytes 1179656 | tf_op jit(solution)/shard_map/cond/branch_10_fun/ppermute | solution.py:597
  137.2 40.3 %collective-permute-start.54 = (bf16[384,2,2,128]{3,2,1,0:T(2,128)(2,1)}, bf16[384,2,2,128]{3,2,1,0:T(2,128)(2,1)S(1)}, u32[]{:S(2)}, u32[]{:S(2)}) collective-permute-start(bf16[384,2,2,128]{3,2,1,0:T(2,128)(2,1)} %get-tuple-element.698), channel_id=1, source_target_pairs={{0,2},{1,3},{2,0},{3,1},{4,6},{5,7},{6,4},{7,5},{8,10},{9,11},{10,... | collective-permute-start | bytes 1179656 | tf_op jit(solution)/shard_map/cond/branch_10_fun/ppermute | solution.py:597
  180.1 135.9 %collective-permute-start.156 = (bf16[2048,2,2,128]{3,2,1,0:T(2,128)(2,1)}, bf16[2048,2,2,128]{3,2,1,0:T(2,128)(2,1)}, u32[]{:S(2)}, u32[]{:S(2)}) collective-permute-start(bf16[2048,2,2,128]{3,2,1,0:T(2,128)(2,1)} %get-tuple-element.901._), channel_id=1, source_target_pairs={{0,2},{1,3},{2,0},{3,1},{4,6},{5,7},{6,4},{7,5},{8,10},{9,11},{10,... | collective-permute-start | bytes 6291464 | tf_op jit(solution)/shard_map/ppermute | solution.py:540
  180.4 123.7 %collective-permute-start.158 = (bf16[512,2,2,128]{3,2,1,0:T(2,128)(2,1)}, bf16[512,2,2,128]{3,2,1,0:T(2,128)(2,1)}, u32[]{:S(2)}, u32[]{:S(2)}) collective-permute-start(bf16[512,2,2,128]{3,2,1,0:T(2,128)(2,1)} %get-tuple-element.880._), channel_id=1, source_target_pairs={{0,2},{1,3},{2,0},{3,1},{4,6},{5,7},{6,4},{7,5},{8,10},{9,11},{10,... | collective-permute-start | bytes 1572872 | tf_op jit(solution)/shard_map/ppermute | solution.py:540
  182.5 133.6 %collective-permute-start.157 = (bf16[2048,2,2,128]{3,2,1,0:T(2,128)(2,1)}, bf16[2048,2,2,128]{3,2,1,0:T(2,128)(2,1)}, u32[]{:S(2)}, u32[]{:S(2)}) collective-permute-start(bf16[2048,2,2,128]{3,2,1,0:T(2,128)(2,1)} %get-tuple-element.946), channel_id=1, source_target_pairs={{0,3},{1,2},{2,1},{3,0},{4,7},{5,6},{6,5},{7,4},{8,11},{9,10},{10,... | collective-permute-start | bytes 6291464 | tf_op jit(solution)/shard_map/ppermute | solution.py:540
  182.5 121.5 %collective-permute-start.159 = (bf16[512,2,2,128]{3,2,1,0:T(2,128)(2,1)}, bf16[512,2,2,128]{3,2,1,0:T(2,128)(2,1)}, u32[]{:S(2)}, u32[]{:S(2)}) collective-permute-start(bf16[512,2,2,128]{3,2,1,0:T(2,128)(2,1)} %get-tuple-element.947), channel_id=1, source_target_pairs={{0,3},{1,2},{2,1},{3,0},{4,7},{5,6},{6,5},{7,4},{8,11},{9,10},{10,... | collective-permute-start | bytes 1572872 | tf_op jit(solution)/shard_map/ppermute | solution.py:540
  228.7 65.8 %collective-permute-start.141 = (bf16[1,2048]{1,0:T(2,128)(2,1)S(1)}, bf16[1,2048]{1,0:T(2,128)(2,1)}, u32[]{:S(2)}, u32[]{:S(2)}) collective-permute-start(bf16[1,2048]{1,0:T(2,128)(2,1)S(1)} %get-tuple-element.959), channel_id=1, source_target_pairs={{0,3},{1,2},{2,1},{3,0},{4,7},{5,6},{6,5},{7,4},{8,11},{9,10},{10,... | collective-permute-start | bytes 12296 | tf_op jit(solution)/shard_map/ppermute | solution.py:540
  302.6 37.6 %collective-permute-start.149 = (bf16[1536,2,2,128]{3,2,1,0:T(2,128)(2,1)}, bf16[1536,2,2,128]{3,2,1,0:T(2,128)(2,1)}, u32[]{:S(2)}, u32[]{:S(2)}) collective-permute-start(bf16[1536,2,2,128]{3,2,1,0:T(2,128)(2,1)} %get-tuple-element.943), channel_id=1, source_target_pairs={{0,4},{4,0},{8,12},{12,8},{1,5},{5,1},{9,13},{13,9},{2,6},{6,2},{1... | collective-permute-start | bytes 4718600 | tf_op jit(solution)/shard_map/ppermute | solution.py:559
  304.0 70.5 %collective-permute-start.150 = (bf16[1536,2,2,128]{3,2,1,0:T(2,128)(2,1)}, bf16[1536,2,2,128]{3,2,1,0:T(2,128)(2,1)}, u32[]{:S(2)}, u32[]{:S(2)}) collective-permute-start(bf16[1536,2,2,128]{3,2,1,0:T(2,128)(2,1)} %get-tuple-element.944), channel_id=1, source_target_pairs={{0,8},{4,12},{8,0},{12,4},{1,9},{5,13},{9,1},{13,5},{2,10},{6,14},... | collective-permute-start | bytes 4718600 | tf_op jit(solution)/shard_map/ppermute | solution.py:559
  304.0 80.2 %collective-permute-start.151 = (bf16[1536,2,2,128]{3,2,1,0:T(2,128)(2,1)}, bf16[1536,2,2,128]{3,2,1,0:T(2,128)(2,1)}, u32[]{:S(2)}, u32[]{:S(2)}) collective-permute-start(bf16[1536,2,2,128]{3,2,1,0:T(2,128)(2,1)} %get-tuple-element.945), channel_id=1, source_target_pairs={{0,12},{4,8},{8,4},{12,0},{1,13},{5,9},{9,5},{13,1},{2,14},{6,10},... | collective-permute-start | bytes 4718600 | tf_op jit(solution)/shard_map/ppermute | solution.py:559
  316.0 88.5 %collective-permute-start.148 = (bf16[4096,2,2,128]{3,2,1,0:T(2,128)(2,1)}, bf16[4096,2,2,128]{3,2,1,0:T(2,128)(2,1)}, u32[]{:S(2)}, u32[]{:S(2)}) collective-permute-start(bf16[4096,2,2,128]{3,2,1,0:T(2,128)(2,1)} %get-tuple-element.926), channel_id=1, source_target_pairs={{0,1},{1,0},{2,3},{3,2},{4,5},{5,4},{6,7},{7,6},{8,9},{9,8},{10,11... | collective-permute-start | bytes 12582920 | tf_op jit(solution)/shard_map/ppermute | solution.py:540
  316.0 71.0 %collective-permute-start.152 = (bf16[1536,2,2,128]{3,2,1,0:T(2,128)(2,1)}, bf16[1536,2,2,128]{3,2,1,0:T(2,128)(2,1)}, u32[]{:S(2)}, u32[]{:S(2)}) collective-permute-start(bf16[1536,2,2,128]{3,2,1,0:T(2,128)(2,1)} %get-tuple-element.942.refs_0_), channel_id=1, source_target_pairs={{0,1},{1,0},{2,3},{3,2},{4,5},{5,4},{6,7},{7,6},{8,9},{9,8},{10,11... | collective-permute-start | bytes 4718600 | tf_op jit(solution)/shard_map/ppermute | solution.py:540
  340.2 50.1 %collective-permute-start.153 = (bf16[1536,2,2,128]{3,2,1,0:T(2,128)(2,1)}, bf16[1536,2,2,128]{3,2,1,0:T(2,128)(2,1)}, u32[]{:S(2)}, u32[]{:S(2)}) collective-permute-start(bf16[1536,2,2,128]{3,2,1,0:T(2,128)(2,1)} %collective-permute-done.149.refs_1_), channel_id=1, source_target_pairs={{0,1},{1,0},{2,3},{3,2},{4,5},{5,4},{6,7},{7,6},{8,9},{9,8},{10,11... | collective-permute-start | bytes 4718600 | tf_op jit(solution)/shard_map/ppermute | solution.py:540
  384.2 88.0 %collective-permute-start.160 = (bf16[4096,2,2,128]{3,2,1,0:T(2,128)(2,1)}, bf16[4096,2,2,128]{3,2,1,0:T(2,128)(2,1)}, u32[]{:S(2)}, u32[]{:S(2)}) collective-permute-start(bf16[4096,2,2,128]{3,2,1,0:T(2,128)(2,1)} %get-tuple-element.949), channel_id=1, source_target_pairs={{0,1},{1,0},{2,3},{3,2},{4,5},{5,4},{6,7},{7,6},{8,9},{9,8},{10,11... | collective-permute-start | bytes 12582920 | tf_op jit(solution)/shard_map/ppermute | solution.py:540
  387.0 44.5 %collective-permute-start.165 = (bf16[1792,2,2,128]{3,2,1,0:T(2,128)(2,1)}, bf16[1792,2,2,128]{3,2,1,0:T(2,128)(2,1)}, u32[]{:S(2)}, u32[]{:S(2)}) collective-permute-start(bf16[1792,2,2,128]{3,2,1,0:T(2,128)(2,1)} %get-tuple-element.954._), channel_id=1, source_target_pairs={{0,2},{1,3},{2,0},{3,1},{4,6},{5,7},{6,4},{7,5},{8,10},{9,11},{10,... | collective-permute-start | bytes 5505032 | tf_op jit(solution)/shard_map/ppermute | solution.py:540
  390.3 80.0 %collective-permute-start.166 = (bf16[1792,2,2,128]{3,2,1,0:T(2,128)(2,1)}, bf16[1792,2,2,128]{3,2,1,0:T(2,128)(2,1)}, u32[]{:S(2)}, u32[]{:S(2)}) collective-permute-start(bf16[1792,2,2,128]{3,2,1,0:T(2,128)(2,1)} %get-tuple-element.955), channel_id=1, source_target_pairs={{0,3},{1,2},{2,1},{3,0},{4,7},{5,6},{6,5},{7,4},{8,11},{9,10},{10,... | collective-permute-start | bytes 5505032 | tf_op jit(solution)/shard_map/ppermute | solution.py:540
  402.5 83.3 %collective-permute-start.163 = (bf16[512,2,2,128]{3,2,1,0:T(2,128)(2,1)}, bf16[512,2,2,128]{3,2,1,0:T(2,128)(2,1)}, u32[]{:S(2)}, u32[]{:S(2)}) collective-permute-start(bf16[512,2,2,128]{3,2,1,0:T(2,128)(2,1)} %get-tuple-element.952._), channel_id=1, source_target_pairs={{0,2},{1,3},{2,0},{3,1},{4,6},{5,7},{6,4},{7,5},{8,10},{9,11},{10,... | collective-permute-start | bytes 1572872 | tf_op jit(solution)/shard_map/ppermute | solution.py:540
  404.4 88.4 %collective-permute-start.164 = (bf16[512,2,2,128]{3,2,1,0:T(2,128)(2,1)}, bf16[512,2,2,128]{3,2,1,0:T(2,128)(2,1)}, u32[]{:S(2)}, u32[]{:S(2)}) collective-permute-start(bf16[512,2,2,128]{3,2,1,0:T(2,128)(2,1)} %get-tuple-element.953), channel_id=1, source_target_pairs={{0,3},{1,2},{2,1},{3,0},{4,7},{5,6},{6,5},{7,4},{8,11},{9,10},{10,... | collective-permute-start | bytes 1572872 | tf_op jit(solution)/shard_map/ppermute | solution.py:540
  431.5 67.4 %collective-permute-start.161 = (bf16[256,2,2,128]{3,2,1,0:T(2,128)(2,1)}, bf16[256,2,2,128]{3,2,1,0:T(2,128)(2,1)}, u32[]{:S(2)}, u32[]{:S(2)}) collective-permute-start(bf16[256,2,2,128]{3,2,1,0:T(2,128)(2,1)} %get-tuple-element.950), channel_id=1, source_target_pairs={{0,2},{1,3},{2,0},{3,1},{4,6},{5,7},{6,4},{7,5},{8,10},{9,11},{10,... | collective-permute-start | bytes 786440 | tf_op jit(solution)/shard_map/ppermute | solution.py:540
  470.3 32.8 %collective-permute-start.162 = (bf16[256,2,2,128]{3,2,1,0:T(2,128)(2,1)}, bf16[256,2,2,128]{3,2,1,0:T(2,128)(2,1)}, u32[]{:S(2)}, u32[]{:S(2)}) collective-permute-start(bf16[256,2,2,128]{3,2,1,0:T(2,128)(2,1)} %get-tuple-element.951), channel_id=1, source_target_pairs={{0,3},{1,2},{2,1},{3,0},{4,7},{5,6},{6,5},{7,4},{8,11},{9,10},{10,... | collective-permute-start | bytes 786440 | tf_op jit(solution)/shard_map/ppermute | solution.py:540
  (14 other events, 443.0 us)
